TPU v7x, 32 devices: a whole 2x2x4 slice. The times are simulated.
32 devices in a mesh: data: 2 (over x), model: 16 (over z, y, core).
Axes of the slice: x: 2, y: 2, z: 4, core: 2. Of those that a mesh axis runs over, the one named last changes fastest.
Arguments:
- x_in: bfloat16 [2, 256, 4096], P('data'), parts along dimension 0
- seg_ids: int32 [2, 256], P('data'), parts along dimension 0
- gain_one: bfloat16 [4096], replicated
- w_qkv: bfloat16 [4096, 12288], P(None, 'model')
- w_out: bfloat16 [32, 128, 4096], P('model')
- gain_two: bfloat16 [4096], replicated
- w_up: bfloat16 [4096, 14336], P(None, 'model')
- w_down: bfloat16 [14336, 4096], P('model')
- d_y: bfloat16 [2, 256, 4096], P('data'), parts along dimension 0
Outputs:
- output 1: bfloat16 [2, 256, 4096], P('data'), parts along dimension 0
- output 2: bfloat16 [2, 256, 4096], P('data'), parts along dimension 0
- output 3: bfloat16 [8192, 12288], P('data', 'model'), parts along dimension 0
- output 4: bfloat16 [64, 128, 4096], P(('data', 'model')), parts along dimension 0
- output 5: bfloat16 [8192, 14336], P('data', 'model'), parts along dimension 0
- output 6: bfloat16 [28672, 4096], P(('data', 'model')), parts along dimension 0
- output 7: bfloat16 [8192], P('data'), parts along dimension 0
- output 8: bfloat16 [8192], P('data'), parts along dimension 0
There are 2 independent parts. A program takes and returns all parts, laid end to end along the dimension named above; an argument that names none is the same for every part.
All inputs are finite; a program needn't handle non-finite values.
Results may differ from a plain program's by a relative error of at most 0.02.
Values are sent between devices in bfloat16 or wider.
A program may use at most 1 GiB of HBM per device.

v0:
```python
import jax
import jax.numpy as jnp
from jax import lax
from jax.sharding import PartitionSpec as P

LN_EPS = 1e-5


def layer_norm(x_in, gain):
    x_wide = x_in.astype(jnp.float32)
    row_mean = jnp.mean(x_wide, axis=-1, keepdims=True)
    centered = x_wide - row_mean
    row_var = jnp.mean(centered * centered, axis=-1, keepdims=True)
    return (centered * lax.rsqrt(row_var + LN_EPS) * gain.astype(jnp.float32)).astype(jnp.bfloat16)


def gelu_tanh(up_proj):
    return jax.nn.gelu(up_proj.astype(jnp.float32), approximate=True).astype(jnp.bfloat16)


def block_mask(seg_ids, start, stop):
    q_pos = jnp.arange(start, stop)
    k_pos = jnp.arange(stop)
    causal = q_pos[:, None] >= k_pos[None, :]
    same_doc = seg_ids[:, start:stop, None] == seg_ids[:, None, :stop]
    return (causal[None] & same_doc)[:, None]


def attention_forward(q_all, k_all, v_all, seg_ids, block_len):
    seq_len = q_all.shape[1]
    score_scale = q_all.shape[-1] ** -0.5
    outputs = []
    log_sums = []
    for start in range(0, seq_len, block_len):
        stop = start + block_len
        scores = jnp.einsum('bqnd,bknd->bnqk', q_all[:, start:stop], k_all[:, :stop], preferred_element_type=jnp.float32) * score_scale
        scores = jnp.where(block_mask(seg_ids, start, stop), scores, -1e30)
        row_max = jnp.max(scores, axis=-1, keepdims=True)
        exp_scores = jnp.exp(scores - row_max)
        row_sum = jnp.sum(exp_scores, axis=-1, keepdims=True)
        attn_prob = (exp_scores / row_sum).astype(jnp.bfloat16)
        outputs.append(jnp.einsum('bnqk,bknd->bqnd', attn_prob, v_all[:, :stop], preferred_element_type=jnp.float32).astype(jnp.bfloat16))
        log_sums.append(row_max + jnp.log(row_sum))
    return jnp.concatenate(outputs, axis=1), log_sums


def attention_backward(q_all, k_all, v_all, d_attn, seg_ids, log_sums, block_len):
    seq_len = q_all.shape[1]
    score_scale = q_all.shape[-1] ** -0.5
    d_q_blocks = []
    d_k_sum = jnp.zeros(k_all.shape, jnp.float32)
    d_v_sum = jnp.zeros(v_all.shape, jnp.float32)
    for index, start in enumerate(range(0, seq_len, block_len)):
        stop = start + block_len
        q_blk = q_all[:, start:stop]
        d_out_blk = d_attn[:, start:stop]
        scores = jnp.einsum('bqnd,bknd->bnqk', q_blk, k_all[:, :stop], preferred_element_type=jnp.float32) * score_scale
        scores = jnp.where(block_mask(seg_ids, start, stop), scores, -1e30)
        attn_prob = jnp.exp(scores - log_sums[index])
        d_prob = jnp.einsum('bqnd,bknd->bnqk', d_out_blk, v_all[:, :stop], preferred_element_type=jnp.float32)
        d_score = attn_prob * (d_prob - jnp.sum(attn_prob * d_prob, axis=-1, keepdims=True)) * score_scale
        d_score = d_score.astype(jnp.bfloat16)
        d_q_blocks.append(jnp.einsum('bnqk,bknd->bqnd', d_score, k_all[:, :stop], preferred_element_type=jnp.float32).astype(jnp.bfloat16))
        pad_width = ((0, 0), (0, seq_len - stop), (0, 0), (0, 0))
        d_k_blk = jnp.einsum('bnqk,bqnd->bknd', d_score, q_blk, preferred_element_type=jnp.float32)
        d_v_blk = jnp.einsum('bnqk,bqnd->bknd', attn_prob.astype(jnp.bfloat16), d_out_blk, preferred_element_type=jnp.float32)
        d_k_sum = d_k_sum + jnp.pad(d_k_blk, pad_width)
        d_v_sum = d_v_sum + jnp.pad(d_v_blk, pad_width)
    return jnp.concatenate(d_q_blocks, axis=1), d_k_sum.astype(jnp.bfloat16), d_v_sum.astype(jnp.bfloat16)


def solution(mesh):
    def local_step(x_in, seg_ids, gain_one, w_qkv, w_out, gain_two, w_up, w_down, d_y):
        rows, seq_len = x_in.shape[:2]
        n_local, head_dim = w_out.shape[:2]
        block_len = min(seq_len, 256)
        normed_one, ln_one_pull = jax.vjp(layer_norm, x_in, gain_one)
        qkv_proj = jnp.einsum('bsh,hc->bsc', normed_one, w_qkv, preferred_element_type=jnp.float32).astype(jnp.bfloat16)
        qkv_heads = qkv_proj.reshape(rows, seq_len, n_local, 3, head_dim)
        q_all = qkv_heads[:, :, :, 0]
        k_all = qkv_heads[:, :, :, 1]
        v_all = qkv_heads[:, :, :, 2]
        attn_out, log_sums = attention_forward(q_all, k_all, v_all, seg_ids, block_len)
        part_one = jnp.einsum('bsnd,ndh->bsh', attn_out, w_out, preferred_element_type=jnp.float32).astype(jnp.bfloat16)
        sum_one = lax.psum(part_one, 'model')
        resid = (x_in.astype(jnp.float32) + sum_one.astype(jnp.float32)).astype(jnp.bfloat16)
        normed_two, ln_two_pull = jax.vjp(layer_norm, resid, gain_two)
        up_proj = jnp.einsum('bsh,hf->bsf', normed_two, w_up, preferred_element_type=jnp.float32).astype(jnp.bfloat16)
        gelu_out, gelu_pull = jax.vjp(gelu_tanh, up_proj)
        part_two = jnp.einsum('bsf,fh->bsh', gelu_out, w_down, preferred_element_type=jnp.float32).astype(jnp.bfloat16)
        sum_two = lax.psum(part_two, 'model')
        y_out = (resid.astype(jnp.float32) + sum_two.astype(jnp.float32)).astype(jnp.bfloat16)
        d_w_down = jnp.einsum('bsf,bsh->fh', gelu_out, d_y, preferred_element_type=jnp.float32).astype(jnp.bfloat16)
        d_gelu = jnp.einsum('bsh,fh->bsf', d_y, w_down, preferred_element_type=jnp.float32).astype(jnp.bfloat16)
        (d_up,) = gelu_pull(d_gelu)
        d_w_up = jnp.einsum('bsh,bsf->hf', normed_two, d_up, preferred_element_type=jnp.float32).astype(jnp.bfloat16)
        d_norm_part = jnp.einsum('bsf,hf->bsh', d_up, w_up, preferred_element_type=jnp.float32).astype(jnp.bfloat16)
        d_norm_two = lax.psum(d_norm_part, 'model')
        d_resid_ln, d_gain_two = ln_two_pull(d_norm_two)
        d_resid = d_y + d_resid_ln
        d_w_out = jnp.einsum('bsnd,bsh->ndh', attn_out, d_resid, preferred_element_type=jnp.float32).astype(jnp.bfloat16)
        d_attn = jnp.einsum('bsh,ndh->bsnd', d_resid, w_out, preferred_element_type=jnp.float32).astype(jnp.bfloat16)
        d_q, d_k, d_v = attention_backward(q_all, k_all, v_all, d_attn, seg_ids, log_sums, block_len)
        d_qkv = jnp.stack([d_q, d_k, d_v], axis=3).reshape(rows, seq_len, 3 * n_local * head_dim)
        d_w_qkv = jnp.einsum('bsh,bsc->hc', normed_one, d_qkv, preferred_element_type=jnp.float32).astype(jnp.bfloat16)
        d_input_part = jnp.einsum('bsc,hc->bsh', d_qkv, w_qkv, preferred_element_type=jnp.float32).astype(jnp.bfloat16)
        d_norm_one = lax.psum(d_input_part, 'model')
        d_x_ln, d_gain_one = ln_one_pull(d_norm_one)
        d_x = d_resid + d_x_ln
        return y_out, d_x, d_w_qkv, d_w_out, d_w_up, d_w_down, d_gain_one, d_gain_two

    in_specs = (P('data'), P('data'), P(), P(None, 'model'), P('model'), P(), P(None, 'model'), P('model'), P('data'))
    out_specs = (P('data'), P('data'), P('data', 'model'), P(('data', 'model')), P('data', 'model'), P(('data', 'model')), P('data'), P('data'))
    return jax.shard_map(local_step, mesh=mesh, in_specs=in_specs, out_specs=out_specs, check_vma=False)
```

profile of v0, /device:TPU:0, one launch (start us, length us, event | category | flops | bytes accessed | tf_op | source)
XLA Modules:
  0.0 391.5 jit_solution(15914376255526251424)
XLA Ops:
  7.3 2.1 convert_reduce_fusion.1
  9.4 2.3 fusion.22
  11.8 4.7 %convolution_convert_fusion.8 = bf16[256,768]{1,0:T(8,128)(2,1)S(1)} fusion(bf16[4096,768]{1,0:T(8,128)(2,1)} %param.12, bf16[1,256,4096]{2,1,0:T(8,128)(2,1)S(1)} %copy-done.1, f32[4096]{0:T(1024)S(1)} %convert_element_type.167, f32[256]{0:T(256)S(1)} %fusion.86, f32[256]{0:T(256)S(1)} %broadcast_multiply_fusion.1), kind=kOutput, calls=%fused_computation.71 | convolution fusion | flops 1616052224 | bytes 8800256 | tf_op jit(solution)/shard_map/bsh,hc->bsc/dot_general | solution.py:78
  18.0 2.1 fusion.13
  20.4 100.1 %all-reduce.5.cloned.1.call-done = bf16[1,256,4096]{2,1,0:T(8,128)(2,1)} async-done(((bf16[1,256,4096]{2,1,0:T(8,128)(2,1)}), bf16[1,256,4096]{2,1,0:T(8,128)(2,1)}) %all-reduce.5.cloned.1.call-update) | async-done | bytes 2097168 | tf_op jit(solution)/shard_map/psum | solution.py:85
  120.5 3.0 convert_reduce_fusion
  124.9 6.3 %convolution_convert_fusion.7 = bf16[256,896]{1,0:T(8,128)(2,1)S(1)} fusion(bf16[4096,896]{1,0:T(8,128)(2,1)} %param.15, bf16[1,256,4096]{2,1,0:T(8,128)(2,1)S(1)} %get-tuple-element.15, f32[4096]{0:T(1024)S(1)} %convert_element_type.179, f32[256]{0:T(256)S(1)} %fusion.87, f32[256]{0:T(256)S(1)} %broadcast_multiply_fusion), kind=kOutput, calls=%fused_computation.70 | convolution fusion | flops 1884520448 | bytes 9914368 | tf_op jit(solution)/shard_map/bsh,hf->bsf/dot_general | solution.py:88
  131.6 3.0 fusion.61
  135.4 3.7 fusion.15
  139.6 6.9 %fusion.14 = bf16[1,256,4096]{2,1,0:T(8,128)(2,1)} fusion(bf16[896,4096]{1,0:T(8,128)(2,1)} %param.16, bf16[256,896]{1,0:T(8,128)(2,1)S(1)} %convolution_convert_fusion.7), kind=kOutput, calls=%fused_computation.34 | convolution fusion | flops 1882390528 | bytes 9895936 | tf_op jit(solution)/shard_map/bsf,fh->bsh/dot_general | solution.py:90
  146.5 89.7 %all-reduce.7.cloned.1.call-done = bf16[1,256,4096]{2,1,0:T(8,128)(2,1)} async-done(((bf16[1,256,4096]{2,1,0:T(8,128)(2,1)}), bf16[1,256,4096]{2,1,0:T(8,128)(2,1)}) %all-reduce.7.cloned.1.call-update) | async-done | bytes 2097168 | tf_op jit(solution)/shard_map/psum | solution.py:98
  236.2 3.3 fusion.26
  239.7 2.6 fusion.20
  242.3 2.5 fusion.30
  248.8 2.2 fusion.56
  251.1 2.2 fusion.57
  254.4 6.0 %fusion.12 = bf16[1,256,4096]{2,1,0:T(8,128)(2,1)} fusion(bf16[256,768]{0,1:T(8,128)(2,1)S(1)} %bitcast.111, bf16[4096,768]{1,0:T(8,128)(2,1)} %param.12), kind=kOutput, calls=%fused_computation.32 | convolution fusion | flops 1611661312 | bytes 8781824 | tf_op jit(solution)/shard_map/bsc,hc->bsh/dot_general | solution.py:106
  260.4 7.3 %convolution_convert_fusion = bf16[896,4096]{1,0:T(8,128)(2,1)} fusion(bf16[1,256,4096]{2,1,0:T(8,128)(2,1)} %param.17, bf16[256,896]{1,0:T(8,128)(2,1)S(1)} %convolution_convert_fusion.7), kind=kOutput, calls=%fused_computation.1 | convolution fusion | flops 1885011968 | bytes 9895936 | tf_op jit(solution)/shard_map/bsf,bsh->fh/dot_general | solution.py:93
  267.8 5.8 %convolution_convert_fusion.1 = bf16[4096,896]{1,0:T(8,128)(2,1)} fusion(bf16[256,896]{1,0:T(8,128)(2,1)S(1)} %copy-done.21, bf16[1,256,4096]{2,1,0:T(8,128)(2,1)S(1)} %copy-done.6, f32[4096]{0:T(1024)S(1)} %convert_element_type.179, f32[256]{0:T(256)S(1)} %fusion.87, f32[256]{0:T(256)S(1)} %broadcast_multiply_fusion), kind=kOutput, calls=%fused_computation.2 | convolution fusion | flops 1887961088 | bytes 9914368 | tf_op jit(solution)/shard_map/bsh,bsf->hf/dot_general | solution.py:96
  275.6 5.0 %convolution_convert_fusion.2 = bf16[4096,768]{1,0:T(8,128)(2,1)} fusion(bf16[256,768]{0,1:T(8,128)(2,1)S(1)} %bitcast.112, bf16[1,256,4096]{2,1,0:T(8,128)(2,1)S(1)} %copy-done.2, f32[4096]{0:T(1024)S(1)} %convert_element_type.167, f32[256]{0:T(256)S(1)} %fusion.86, f32[256]{0:T(256)S(1)} %broadcast_multiply_fusion.1), kind=kOutput, calls=%fused_computation.3 | convolution fusion | flops 1619001344 | bytes 8800256 | tf_op jit(solution)/shard_map/bsh,bsc->hc/dot_general | solution.py:105
  280.6 90.6 %all-reduce.9.cloned.1.call-done = (bf16[1,256,4096]{2,1,0:T(8,128)(2,1)}, bf16[1,256,4096]{2,1,0:T(8,128)(2,1)}) async-done(((bf16[1,256,4096]{2,1,0:T(8,128)(2,1)}, bf16[1,256,4096]{2,1,0:T(8,128)(2,1)}), (bf16[1,256,4096]{2,1,0:T(8,128)(2,1)}, bf16[1,256,4096]{2,1,0:T(8,128)(2,1)})) %all-reduce.9.cloned.1.call-update) | async-done | bytes 4194320 | tf_op jit(solution)/shard_map/psum | solution.py:91
  371.2 3.3 fusion.23
  374.6 6.3 %fusion.21 = (bf16[4096]{0:T(1024)(128)(2,1)}, f32[256]{0:T(256)S(1)}, bf16[1,256,4096]{2,1,0:T(8,128)(2,1)}) fusion(bf16[1,256,4096]{2,1,0:T(8,128)(2,1)} %get-tuple-element.13, bf16[1,256,4096]{2,1,0:T(8,128)(2,1)S(1)} %copy-done.3, f32[256]{0:T(256)S(1)} %fusion.86, f32[256]{0:T(256)S(1)} %broadcast_multiply_fusion.1, f32[256]{0:T(256)S(1)} %multiply_multiply_fusion, ...), kind=kLoop, calls=%fused_computation.41 | loop fusion | flops 16772864 | bytes 10514432 | tf_op jit(solution)/shard_map/transpose(jvp())/reduce_sum | solution.py:14
  381.0 3.8 fusion.31
  (83 shorter events, 12.4 us)
Async XLA Ops:
  7.2 10.9 %copy-start = (bf16[2,128,4096]{2,1,0:T(8,128)(2,1)S(1)}, bf16[2,128,4096]{2,1,0:T(8,128)(2,1)}, u32[]{:S(2)}) copy-start(bf16[2,128,4096]{2,1,0:T(8,128)(2,1)} %param.13) | copy-start | bytes 6291460
  7.2 4.5 %copy-start.17 = (bf16[4096]{0:T(1024)(128)(2,1)S(1)}, bf16[4096]{0:T(1024)(128)(2,1)}, u32[]{:S(2)}) copy-start(bf16[4096]{0:T(1024)(128)(2,1)} %param.11) | copy-start | bytes 24580
  7.2 4.5 %copy-start.19 = (s32[1,256]{1,0:T(1,128)S(1)}, s32[1,256]{1,0:T(1,128)}, u32[]{:S(2)}) copy-start(s32[1,256]{1,0:T(1,128)} %param.10) | copy-start | bytes 3076
  7.2 113.3 %all-reduce.5.cloned.1.call-start = ((), (), s32[]{:S(2)}) async-start(), calls=%async_computation | async-start | bytes 4194304 | tf_op jit(solution)/shard_map/psum | solution.py:85
  7.2 4.6 %copy-start.1 = (bf16[1,256,4096]{2,1,0:T(8,128)(2,1)S(1)}, bf16[1,256,4096]{2,1,0:T(8,128)(2,1)}, u32[]{:S(2)}) copy-start(bf16[1,256,4096]{2,1,0:T(8,128)(2,1)} %param.9) | copy-start | bytes 6291460
  17.1 3.3 copy-start.18
  20.1 216.1 %all-reduce.7.cloned.1.call-start = ((), (), s32[]{:S(2)}) async-start(), calls=%async_computation.1 | async-start | bytes 4194304 | tf_op jit(solution)/shard_map/psum | solution.py:98
  123.6 7.6 %slice-start.2 = ((s8[7340032]{0:T(1024)(128)(4,1)}), s8[4194304]{0:T(1024)(128)(4,1)S(1)}, s32[]{:S(2)}) async-start(s8[7340032]{0:T(1024)(128)(4,1)} %bitcast.116), calls=%async_computation.5 | async-start | bytes 8388608
  123.6 11.7 %slice-start = ((s8[7340032]{0:T(1024)(128)(4,1)}), s8[4194304]{0:T(1024)(128)(4,1)S(1)}, s32[]{:S(2)}) async-start(s8[7340032]{0:T(1024)(128)(4,1)} %bitcast.114), calls=%async_computation.3 | async-start | bytes 8388608
  124.9 6.3 %copy-start.13 = (bf16[1,256,4096]{2,1,0:T(8,128)(2,1)S(1)}, bf16[1,256,4096]{2,1,0:T(8,128)(2,1)}, u32[]{:S(2)}) copy-start(bf16[1,256,4096]{2,1,0:T(8,128)(2,1)} %param.17) | copy-start | bytes 6291460
  124.9 6.7 %slice-start.3 = ((s8[7340032]{0:T(1024)(128)(4,1)}), s8[3145728]{0:T(1024)(128)(4,1)S(1)}, s32[]{:S(2)}) async-start(s8[7340032]{0:T(1024)(128)(4,1)} %bitcast.116), calls=%async_computation.6 | async-start | bytes 6291456
  124.9 10.5 %slice-start.1 = ((s8[7340032]{0:T(1024)(128)(4,1)}), s8[3145728]{0:T(1024)(128)(4,1)S(1)}, s32[]{:S(2)}) async-start(s8[7340032]{0:T(1024)(128)(4,1)} %bitcast.114), calls=%async_computation.4 | async-start | bytes 6291456
  139.1 232.1 %all-reduce.9.cloned.1.call-start = ((), (), s32[]{:S(2)}) async-start(), calls=%async_computation.2 | async-start | bytes 8388608 | tf_op jit(solution)/shard_map/psum | solution.py:91
  236.2 3.4 copy-start.5
  236.2 3.5 copy-start.8
  236.2 6.1 %copy-start.14 = (bf16[1,256,4096]{2,1,0:T(8,128)(2,1)S(1)}, bf16[1,256,4096]{2,1,0:T(8,128)(2,1)}, u32[]{:S(2)}) copy-start(bf16[1,256,4096]{2,1,0:T(8,128)(2,1)} %param.17) | copy-start | bytes 6291460
  260.4 7.4 %copy-start.6 = (bf16[1,256,4096]{2,1,0:T(8,128)(2,1)S(1)}, bf16[1,256,4096]{2,1,0:T(8,128)(2,1)}, u32[]{:S(2)}) copy-start(bf16[1,256,4096]{2,1,0:T(8,128)(2,1)} %copy-done.4) | copy-start | bytes 6291460
  260.4 7.4 %copy-start.21 = (bf16[256,896]{1,0:T(8,128)(2,1)S(1)}, bf16[256,896]{1,0:T(8,128)(2,1)}, u32[]{:S(2)}) copy-start(bf16[256,896]{1,0:T(8,128)(2,1)} %copy-done.20) | copy-start | bytes 1376260
  267.8 5.8 %copy-start.10 = (bf16[1,256,4096]{2,1,0:T(8,128)(2,1)S(1)}, bf16[1,256,4096]{2,1,0:T(8,128)(2,1)}, u32[]{:S(2)}) copy-start(bf16[1,256,4096]{2,1,0:T(8,128)(2,1)} %copy-done.9) | copy-start | bytes 6291460
  267.8 5.8 %copy-start.16 = (bf16[256,2,128]{0,2,1:T(8,128)(2,1)S(1)}, bf16[256,2,128]{0,2,1:T(8,128)(2,1)}, u32[]{:S(2)}) copy-start(bf16[256,2,128]{0,2,1:T(8,128)(2,1)} %copy-done.15) | copy-start | bytes 393220
  371.1 3.4 copy-start.3
  371.2 3.5 copy-start.7
  374.6 6.4 %copy-start.11 = (bf16[1,256,4096]{2,1,0:T(8,128)(2,1)S(1)}, bf16[1,256,4096]{2,1,0:T(8,128)(2,1)}, u32[]{:S(2)}) copy-start(bf16[1,256,4096]{2,1,0:T(8,128)(2,1)} %copy-done.9) | copy-start | bytes 6291460
  374.6 6.4 %copy-start.12 = (bf16[1,256,4096]{2,1,0:T(8,128)(2,1)S(1)}, bf16[1,256,4096]{2,1,0:T(8,128)(2,1)}, u32[]{:S(2)}) copy-start(bf16[1,256,4096]{2,1,0:T(8,128)(2,1)} %get-tuple-element.13) | copy-start | bytes 6291460
  (5 other events, 6.1 us)
Sparse Core Ops, SparseCore 0:
  20.2 100.2 all-reduce.4
  139.2 96.9 all-reduce.6
  260.5 110.5 all-reduce.8
where the time goes:
time: 395 us; the launch traced here: 391 us
  waiting for transfers between devices  280 us (71%)
  matrix products  60.4 us (15%)
  other arithmetic  31.3 us (8%)
  between operations  14.2 us (4%)
  local copies, waits for them, and re-layouts  4.24 us (1%)
    psum x1, waiting for transfers between devices, local_step(): sum_one = lax.psum(part_one, 'model')  100 us
    psum x1, waiting for transfers between devices, local_step(): sum_two = lax.psum(part_two, 'model')  90.6 us
    psum x1, waiting for transfers between devices, local_step(): d_norm_two = lax.psum(d_norm_part, 'model')  89.7 us
    reduce_sum x4, other arithmetic, layer_norm(): centered * lax.rsqrt(row_var + LN_EPS) * gain.astype(jnp.float32)  15.6 us
  transfers between devices with their start and end apart: 3, of which 3 were waited for; matrix products, arithmetic and copies ran while one was open for 7% of the time, Pallas kernels for 0%

commit v1 on v0

--- a/solution.py
+++ b/solution.py
@@ -1,9 +1,141 @@
+import functools
+
 import jax
 import jax.numpy as jnp
 from jax import lax
+from jax.experimental import pallas as pl
+from jax.experimental.pallas import tpu as pltpu
 from jax.sharding import PartitionSpec as P
 
 LN_EPS = 1e-5
+MESH = pl.DeviceIdType.MESH
+COLS = 1024
+
+
+def flip(z, k):
+    return (z // 2 + k // 2) % 2 * 2 + (z % 2 + k % 2) % 2
+
+
+def all_reduce_kernel(part, full, buf_core, buf_y, out_y, sum_z, buf_z, send_core, recv_core, send_y, recv_y, send_z, recv_z, gat_zs, gat_zr, gat_ys, gat_yr, gat_cs, gat_cr):
+    me = lax.axis_index('model')
+    core, y_pos, z_pos = me % 2, me // 2 % 2, me // 4
+
+    def device(z, y, c):
+        return {'model': (z * 2 + y) * 2 + c}
+
+    def block(c, y, z):
+        return c * 8 + y * 4 + z
+
+    def copy(src, dst, s, r, dev):
+        return pltpu.make_async_remote_copy(src_ref=src, dst_ref=dst, send_sem=s, recv_sem=r, device_id=dev, device_id_type=MESH)
+
+    partner = device(z_pos, y_pos, 1 - core)
+    y_peer = device(z_pos, 1 - y_pos, core)
+    z_peers = [None] + [device(flip(z_pos, k), y_pos, core) for k in (1, 2, 3)]
+
+    barrier = pltpu.get_barrier_semaphore()
+    for dev in [partner, y_peer] + z_peers[1:]:
+        pl.semaphore_signal(barrier, inc=1, device_id=dev, device_id_type=MESH)
+    pl.semaphore_wait(barrier, 5)
+
+    def by_columns(body):
+        def step(i, carry):
+            body(pl.ds(pl.multiple_of(i * COLS, COLS), COLS))
+            return carry
+        lax.fori_loop(0, 4096 // COLS, step, 0)
+
+    core_copies, y_copies, z_copies = {}, {}, {}
+    for k in (3, 2, 1, 0):
+        z_to = flip(z_pos, k)
+        for j in (1, 0):
+            y_to = (y_pos + j) % 2
+            cp = copy(part.at[block(1 - core, y_to, z_to)], buf_core.at[k, j], send_core.at[k, j], recv_core.at[k, j], partner)
+            cp.start()
+            core_copies[k, j] = cp
+    for k in (3, 2, 1, 0):
+        z_to = flip(z_pos, k)
+        core_copies[k, 1].wait_recv()
+        mine = block(core, 1 - y_pos, z_to)
+
+        def add_core(c, k=k, mine=mine):
+            out_y[k, :, c] = (part[mine, :, c].astype(jnp.float32) + buf_core[k, 1, :, c].astype(jnp.float32)).astype(jnp.bfloat16)
+        by_columns(add_core)
+        cp = copy(out_y.at[k], buf_y.at[k], send_y.at[k], recv_y.at[k], y_peer)
+        cp.start()
+        y_copies[k] = cp
+    for k in (3, 2, 1):
+        z_to = flip(z_pos, k)
+        core_copies[k, 0].wait_recv()
+        y_copies[k].wait_recv()
+        mine = block(core, y_pos, z_to)
+
+        def add_y(c, k=k, mine=mine):
+            sum_z[k - 1, :, c] = (part[mine, :, c].astype(jnp.float32) + buf_core[k, 0, :, c].astype(jnp.float32) + buf_y[k, :, c].astype(jnp.float32)).astype(jnp.bfloat16)
+        by_columns(add_y)
+        cp = copy(sum_z.at[k - 1], buf_z.at[k - 1], send_z.at[k - 1], recv_z.at[k - 1], z_peers[k])
+        cp.start()
+        z_copies[k] = cp
+    core_copies[0, 0].wait_recv()
+    y_copies[0].wait_recv()
+    for k in (3, 2, 1):
+        z_copies[k].wait_recv()
+    own = block(core, y_pos, z_pos)
+
+    def add_all(c):
+        total = part[own, :, c].astype(jnp.float32) + buf_core[0, 0, :, c].astype(jnp.float32) + buf_y[0, :, c].astype(jnp.float32)
+        for k in (3, 2, 1):
+            total = total + buf_z[k - 1, :, c].astype(jnp.float32)
+        full[own, :, c] = total.astype(jnp.bfloat16)
+    by_columns(add_all)
+
+    gather = []
+
+    def pass_on(b, s, r, dev):
+        cp = copy(full.at[b], full.at[b], s, r, dev)
+        cp.start()
+        gather.append(cp)
+        return cp
+    z_out = {k: pass_on(own, gat_zs.at[k - 1], gat_zr.at[k - 1], z_peers[k]) for k in (3, 2, 1)}
+    y_out = {0: pass_on(own, gat_ys.at[0], gat_yr.at[0], y_peer)}
+    c_out = [pass_on(own, gat_cs.at[0, 0], gat_cr.at[0, 0], partner)]
+    for k in (1, 2, 3):
+        z_out[k].wait_recv()
+        b = block(core, y_pos, flip(z_pos, k))
+        y_out[k] = pass_on(b, gat_ys.at[k], gat_yr.at[k], y_peer)
+        c_out.append(pass_on(b, gat_cs.at[0, k], gat_cr.at[0, k], partner))
+    for k in (0, 1, 2, 3):
+        y_out[k].wait_recv()
+        b = block(core, 1 - y_pos, flip(z_pos, k))
+        c_out.append(pass_on(b, gat_cs.at[1, k], gat_cr.at[1, k], partner))
+    for cp in c_out:
+        cp.wait_recv()
+    for cp in list(core_copies.values()) + list(y_copies.values()) + list(z_copies.values()) + gather:
+        cp.wait_send()
+
+
+def all_reduce(part, ident):
+    blocks = part.reshape(16, 16, 4096)
+    vmem = pl.BlockSpec(memory_space=pltpu.VMEM)
+    dma = pltpu.SemaphoreType.DMA
+    bf16 = jnp.bfloat16
+    out = pl.pallas_call(
+        all_reduce_kernel,
+        out_shape=jax.ShapeDtypeStruct(blocks.shape, bf16),
+        in_specs=[vmem],
+        out_specs=vmem,
+        scratch_shapes=[
+            pltpu.VMEM((4, 2, 16, 4096), bf16),
+            pltpu.VMEM((4, 16, 4096), bf16),
+            pltpu.VMEM((4, 16, 4096), bf16),
+            pltpu.VMEM((3, 16, 4096), bf16),
+            pltpu.VMEM((3, 16, 4096), bf16),
+            dma((4, 2)), dma((4, 2)), dma((4,)), dma((4,)), dma((3,)), dma((3,)),
+            dma((3,)), dma((3,)), dma((4,)), dma((4,)), dma((2, 4)), dma((2, 4)),
+        ],
+        compiler_params=pltpu.CompilerParams(collective_id=ident, has_side_effects=True, vmem_limit_bytes=16 * 2 ** 20),
+        name=f'all_reduce_{ident}',
+    )(blocks)
+    return out.reshape(part.shape)
 
 
 def layer_norm(x_in, gain):
@@ -82,20 +214,20 @@
         v_all = qkv_heads[:, :, :, 2]
         attn_out, log_sums = attention_forward(q_all, k_all, v_all, seg_ids, block_len)
         part_one = jnp.einsum('bsnd,ndh->bsh', attn_out, w_out, preferred_element_type=jnp.float32).astype(jnp.bfloat16)
-        sum_one = lax.psum(part_one, 'model')
+        sum_one = all_reduce(part_one, 0)
         resid = (x_in.astype(jnp.float32) + sum_one.astype(jnp.float32)).astype(jnp.bfloat16)
         normed_two, ln_two_pull = jax.vjp(layer_norm, resid, gain_two)
         up_proj = jnp.einsum('bsh,hf->bsf', normed_two, w_up, preferred_element_type=jnp.float32).astype(jnp.bfloat16)
         gelu_out, gelu_pull = jax.vjp(gelu_tanh, up_proj)
         part_two = jnp.einsum('bsf,fh->bsh', gelu_out, w_down, preferred_element_type=jnp.float32).astype(jnp.bfloat16)
-        sum_two = lax.psum(part_two, 'model')
+        sum_two = all_reduce(part_two, 1)
         y_out = (resid.astype(jnp.float32) + sum_two.astype(jnp.float32)).astype(jnp.bfloat16)
         d_w_down = jnp.einsum('bsf,bsh->fh', gelu_out, d_y, preferred_element_type=jnp.float32).astype(jnp.bfloat16)
         d_gelu = jnp.einsum('bsh,fh->bsf', d_y, w_down, preferred_element_type=jnp.float32).astype(jnp.bfloat16)
         (d_up,) = gelu_pull(d_gelu)
         d_w_up = jnp.einsum('bsh,bsf->hf', normed_two, d_up, preferred_element_type=jnp.float32).astype(jnp.bfloat16)
         d_norm_part = jnp.einsum('bsf,hf->bsh', d_up, w_up, preferred_element_type=jnp.float32).astype(jnp.bfloat16)
-        d_norm_two = lax.psum(d_norm_part, 'model')
+        d_norm_two = all_reduce(d_norm_part, 2)
         d_resid_ln, d_gain_two = ln_two_pull(d_norm_two)
         d_resid = d_y + d_resid_ln
         d_w_out = jnp.einsum('bsnd,bsh->ndh', attn_out, d_resid, preferred_element_type=jnp.float32).astype(jnp.bfloat16)
@@ -104,7 +236,7 @@
         d_qkv = jnp.stack([d_q, d_k, d_v], axis=3).reshape(rows, seq_len, 3 * n_local * head_dim)
         d_w_qkv = jnp.einsum('bsh,bsc->hc', normed_one, d_qkv, preferred_element_type=jnp.float32).astype(jnp.bfloat16)
         d_input_part = jnp.einsum('bsc,hc->bsh', d_qkv, w_qkv, preferred_element_type=jnp.float32).astype(jnp.bfloat16)
-        d_norm_one = lax.psum(d_input_part, 'model')
+        d_norm_one = all_reduce(d_input_part, 3)
         d_x_ln, d_gain_one = ln_one_pull(d_norm_one)
         d_x = d_resid + d_x_ln
         return y_out, d_x, d_w_qkv, d_w_out, d_w_up, d_w_down, d_gain_one, d_gain_two

time: 395 us -> 247 us (0.63)
  waiting for transfers between devices: 280 us -> 0 us
  Pallas kernels: 0 us -> 168 us
  between operations: 14.2 us -> 1.5 us
  matrix products: 60.4 us -> 47.7 us
  other arithmetic: 31.3 us -> 22.9 us
    psum x3 -> x0, waiting for transfers between devices: 280 us -> none  [the longest x1 100 us: local_step(): sum_one = lax.psum(part_one, 'model')]
    pallas_call x0 -> x4, Pallas kernels: none -> 168 us  [all_reduce(): pl.pallas_call(all_reduce_kernel, out_shape=jax.ShapeDtypeStruct(blocks.s...]
    reduce_sum x4, other arithmetic: 15.6 us -> 9.52 us  [layer_norm(): centered * lax.rsqrt(row_var + LN_EPS) * gain.astype(jnp.float32)]
    dot_general x1, matrix products: 6.86 us -> 2.5 us  [local_step(): jnp.einsum('bsf,fh->bsh', gelu_out, w_down, preferred_element_type=jnp.fl...]
  transfers between devices with their start and end apart: 3 -> 0, of which waited for: 3 -> 0; matrix products, arithmetic and copies ran while one was open for 7% -> 0% of each run, Pallas kernels for 0% -> 0%
where the time goes in v1:
time: 247 us; the launch traced here: 243 us
  Pallas kernels  168 us (68%)
  matrix products  47.7 us (19%)
  other arithmetic  22.9 us (9%)
  local copies, waits for them, and re-layouts  2.9 us (1%)
    pallas_call x4, Pallas kernels, all_reduce(): pl.pallas_call(all_reduce_kernel, out_shape=jax.ShapeDtypeStruct(blocks.s...  168 us
    reduce_sum x4, other arithmetic, layer_norm(): centered * lax.rsqrt(row_var + LN_EPS) * gain.astype(jnp.float32)  9.52 us
    dot_general x1, matrix products, local_step(): jnp.einsum('bsh,bsf->hf', normed_two, d_up, preferred_element_type=jnp.fl...  5.82 us
    dot_general x1, matrix products, local_step(): jnp.einsum('bsf,bsh->fh', gelu_out, d_y, preferred_element_type=jnp.float32)  5.41 us

profile of v1, /device:TPU:0, one launch (start us, length us, event | category | flops | bytes accessed | tf_op | source)
XLA Modules:
  0.0 243.3 jit_solution(6509368099828947838)
XLA Ops:
  0.7 2.1 convert_reduce_fusion.1
  2.8 2.3 fusion.18
  5.3 4.7 %convolution_convert_fusion.8 = bf16[256,768]{1,0:T(8,128)(2,1)S(1)} fusion(bf16[4096,768]{1,0:T(8,128)(2,1)} %param.12, bf16[1,256,4096]{2,1,0:T(8,128)(2,1)S(1)} %copy-done.1, f32[4096]{0:T(1024)S(1)} %convert_element_type.219, f32[256]{0:T(256)S(1)} %fusion.82, f32[256]{0:T(256)S(1)} %broadcast_multiply_fusion.1), kind=kOutput, calls=%fused_computation.67 | convolution fusion | flops 1616052224 | bytes 8800256 | tf_op jit(solution)/shard_map/bsh,hc->bsc/dot_general | solution.py:210
  11.6 43.9 %all_reduce_0.1 = bf16[16,16,4096]{2,1,0:T(8,128)(2,1)S(1)} custom-call(bf16[16,16,4096]{2,1,0:T(8,128)(2,1)S(1)} %bitcast.133), custom_call_target="tpu_custom_call" | custom-call | tf_op jit(solution)/shard_map/all_reduce_0/pallas_call | solution.py:121
  57.2 2.5 %convolution_convert_fusion.7 = bf16[256,896]{1,0:T(8,128)(2,1)S(1)} fusion(bf16[4096,896]{1,0:T(8,128)(2,1)S(1)} %bitcast.146, bf16[1,256,4096]{2,1,0:T(8,128)(2,1)S(1)} %get-tuple-element.13, f32[4096]{0:T(1024)S(1)} %convert_element_type.231, f32[256]{0:T(256)S(1)} %fusion.83, f32[256]{0:T(256)S(1)} %broadcast_multiply_fusion), kind=kOutput, calls=%fused_computation.66 | convolution fusion | flops 1884520448 | bytes 9914368 | tf_op jit(solution)/shard_map/bsh,hf->bsf/dot_general | solution.py:220
  61.0 2.8 %fusion.57 = bf16[256,896]{1,0:T(8,128)(2,1)S(1)} fusion(bf16[256,896]{1,0:T(8,128)(2,1)S(1)} %convolution_convert_fusion.7, bf16[896,4096]{1,0:T(8,128)(2,1)S(1)} %bitcast.148, bf16[1,256,4096]{2,1,0:T(8,128)(2,1)S(1)} %copy-done.8), kind=kOutput, calls=%fused_computation.85 | convolution fusion | flops 1884323840 | bytes 10354688 | tf_op jit(solution)/shard_map/bsh,fh->bsf/dot_general | solution.py:226
  63.8 2.4 convolution_convert_fusion.3
  66.1 42.8 %all_reduce_2.1 = bf16[16,16,4096]{2,1,0:T(8,128)(2,1)S(1)} custom-call(bf16[16,16,4096]{2,1,0:T(8,128)(2,1)S(1)} %bitcast.134), custom_call_target="tpu_custom_call" | custom-call | tf_op jit(solution)/shard_map/all_reduce_2/pallas_call | solution.py:121
  110.0 2.5 %convolution_convert_fusion.4 = bf16[256,4096]{1,0:T(8,128)(2,1)S(1)} fusion(bf16[896,4096]{1,0:T(8,128)(2,1)S(1)} %bitcast.148, bf16[256,896]{1,0:T(8,128)(2,1)S(1)} %convolution_convert_fusion.7), kind=kOutput, calls=%fused_computation.26 | convolution fusion | flops 1882390528 | bytes 9895936 | tf_op jit(solution)/shard_map/bsf,fh->bsh/dot_general | solution.py:222
  112.5 40.9 %all_reduce_1.1 = bf16[16,16,4096]{2,1,0:T(8,128)(2,1)S(1)} custom-call(bf16[16,16,4096]{2,1,0:T(8,128)(2,1)S(1)} %bitcast.135), custom_call_target="tpu_custom_call" | custom-call | tf_op jit(solution)/shard_map/all_reduce_1/pallas_call | solution.py:121
  153.4 4.9 %fusion.17 = (bf16[4096]{0:T(1024)(128)(2,1)}, f32[256]{0:T(256)S(1)}, bf16[1,256,4096]{2,1,0:T(8,128)(2,1)}) fusion(bf16[1,256,4096]{2,1,0:T(8,128)(2,1)S(1)} %get-tuple-element.13, f32[256]{0:T(256)S(1)} %fusion.83, f32[256]{0:T(256)S(1)} %broadcast_multiply_fusion, f32[256]{0:T(256)S(1)} %multiply_multiply_fusion.1, f32[4096]{0:T(1024)S(1)} %convert_element_type.231, ...), kind=kLoop, calls=%fused_computation.37 | loop fusion | flops 15724288 | bytes 8417280 | tf_op jit(solution)/shard_map/transpose(jvp())/reduce_sum | solution.py:146
  158.3 2.4 fusion.26
  160.7 1.3 copy-done.6
  164.7 2.2 fusion.52
  166.9 2.2 fusion.53
  169.2 1.1 pad_maximum_fusion
  170.3 3.7 %convolution_convert_fusion.5 = bf16[2,128,4096]{2,1,0:T(8,128)(2,1)} fusion(bf16[256,2,128]{0,2,1:T(8,128)(2,1)} %copy-done.10, bf16[1,256,4096]{2,1,0:T(8,128)(2,1)} %copy-done.6), kind=kOutput, calls=%fused_computation.28 | convolution fusion | flops 537919488 | bytes 4325376 | tf_op jit(solution)/shard_map/bsnd,bsh->ndh/dot_general | solution.py:233
  174.0 4.6 %convolution_convert_fusion.6 = bf16[256,4096]{1,0:T(8,128)(2,1)S(1)} fusion(bf16[256,768]{0,1:T(8,128)(2,1)S(1)} %bitcast.142, bf16[4096,768]{1,0:T(8,128)(2,1)} %param.12), kind=kOutput, calls=%fused_computation.29 | convolution fusion | flops 1611661312 | bytes 8781824 | tf_op jit(solution)/shard_map/bsc,hc->bsh/dot_general | solution.py:238
  178.6 40.7 %all_reduce_3.1 = bf16[16,16,4096]{2,1,0:T(8,128)(2,1)S(1)} custom-call(bf16[16,16,4096]{2,1,0:T(8,128)(2,1)S(1)} %bitcast.136), custom_call_target="tpu_custom_call" | custom-call | tf_op jit(solution)/shard_map/all_reduce_3/pallas_call | solution.py:121
  220.4 2.6 %fusion.16 = (bf16[4096]{0:T(1024)(128)(2,1)}, f32[256]{0:T(256)S(1)}) fusion(bf16[1,256,4096]{2,1,0:T(8,128)(2,1)S(1)} %copy-done.3, f32[256]{0:T(256)S(1)} %fusion.82, f32[256]{0:T(256)S(1)} %broadcast_multiply_fusion.1, f32[256]{0:T(256)S(1)} %multiply_multiply_fusion, f32[4096]{0:T(1024)S(1)} %convert_element_type.219, bf16[1,256,4096]{2,1,0:T(8,128)(2,1)S(1)} %bitcast.129), kind=kLoop, calls=%fused_computation.36 | loop fusion | flops 12578560 | bytes 4222976 | tf_op jit(solution)/shard_map/transpose(jvp())/reduce_sum | solution.py:146
  223.0 3.8 %fusion.27 = bf16[1,256,4096]{2,1,0:T(8,128)(2,1)} fusion(bf16[1,256,4096]{2,1,0:T(8,128)(2,1)S(1)} %copy-done.7, bf16[1,256,4096]{2,1,0:T(8,128)(2,1)S(1)} %copy-done.3, f32[256]{0:T(256)S(1)} %negate_multiply_fusion, f32[256]{0:T(256)S(1)} %multiply_multiply_fusion, f32[4096]{0:T(1024)S(1)} %convert_element_type.219, f32[256]{0:T(256)S(1)} %fusion.82, ...), kind=kLoop, calls=%fused_computation.49 | loop fusion | flops 11534336 | bytes 8409088 | tf_op jit(solution)/shard_map/add | solution.py:241
  226.8 5.8 %convolution_convert_fusion.1 = bf16[4096,896]{1,0:T(8,128)(2,1)} fusion(bf16[256,896]{1,0:T(8,128)(2,1)S(1)} %copy-done.15, bf16[1,256,4096]{2,1,0:T(8,128)(2,1)S(1)} %copy-done.5, f32[4096]{0:T(1024)S(1)} %convert_element_type.231, f32[256]{0:T(256)S(1)} %fusion.83, f32[256]{0:T(256)S(1)} %broadcast_multiply_fusion), kind=kOutput, calls=%fused_computation.2 | convolution fusion | flops 1887961088 | bytes 9914368 | tf_op jit(solution)/shard_map/bsh,bsf->hf/dot_general | solution.py:228
  232.6 4.9 %convolution_convert_fusion.2 = bf16[4096,768]{1,0:T(8,128)(2,1)} fusion(bf16[256,768]{0,1:T(8,128)(2,1)S(1)} %bitcast.143, bf16[1,256,4096]{2,1,0:T(8,128)(2,1)S(1)} %copy-done.3, f32[4096]{0:T(1024)S(1)} %convert_element_type.219, f32[256]{0:T(256)S(1)} %fusion.82, f32[256]{0:T(256)S(1)} %broadcast_multiply_fusion.1), kind=kOutput, calls=%fused_computation.3 | convolution fusion | flops 1619001344 | bytes 8800256 | tf_op jit(solution)/shard_map/bsh,bsc->hc/dot_general | solution.py:237
  237.5 5.4 %convolution_convert_fusion = bf16[896,4096]{1,0:T(8,128)(2,1)} fusion(bf16[1,256,4096]{2,1,0:T(8,128)(2,1)S(1)} %copy-done.9, bf16[256,896]{1,0:T(8,128)(2,1)S(1)} %convolution_convert_fusion.7), kind=kOutput, calls=%fused_computation.1 | convolution fusion | flops 1885011968 | bytes 9895936 | tf_op jit(solution)/shard_map/bsf,bsh->fh/dot_general | solution.py:225
  (66 shorter events, 9.4 us)
Async XLA Ops:
  0.6 10.2 %copy-start = (bf16[2,128,4096]{2,1,0:T(8,128)(2,1)S(1)}, bf16[2,128,4096]{2,1,0:T(8,128)(2,1)}, u32[]{:S(2)}) copy-start(bf16[2,128,4096]{2,1,0:T(8,128)(2,1)} %param.13) | copy-start | bytes 6291460
  0.6 4.6 %copy-start.1 = (bf16[1,256,4096]{2,1,0:T(8,128)(2,1)S(1)}, bf16[1,256,4096]{2,1,0:T(8,128)(2,1)}, u32[]{:S(2)}) copy-start(bf16[1,256,4096]{2,1,0:T(8,128)(2,1)} %param.9) | copy-start | bytes 6291460
  0.7 4.5 %copy-start.12 = (bf16[4096]{0:T(1024)(128)(2,1)S(1)}, bf16[4096]{0:T(1024)(128)(2,1)}, u32[]{:S(2)}) copy-start(bf16[4096]{0:T(1024)(128)(2,1)} %param.14) | copy-start | bytes 24580
  0.7 4.4 %copy-start.11 = (bf16[4096]{0:T(1024)(128)(2,1)S(1)}, bf16[4096]{0:T(1024)(128)(2,1)}, u32[]{:S(2)}) copy-start(bf16[4096]{0:T(1024)(128)(2,1)} %param.11) | copy-start | bytes 24580
  0.7 4.5 %copy-start.13 = (s32[1,256]{1,0:T(1,128)S(1)}, s32[1,256]{1,0:T(1,128)}, u32[]{:S(2)}) copy-start(s32[1,256]{1,0:T(1,128)} %param.10) | copy-start | bytes 3076
  10.8 44.7 %copy-start.10 = (bf16[256,2,128]{0,2,1:T(8,128)(2,1)}, bf16[256,2,128]{0,2,1:T(8,128)(2,1)S(1)}, u32[]{:S(2)}) copy-start(bf16[256,2,128]{0,2,1:T(8,128)(2,1)S(1)} %fusion.51) | copy-start | bytes 393220
  10.8 44.7 %copy-start.2 = (bf16[1,256,4096]{2,1,0:T(8,128)(2,1)S(1)}, bf16[1,256,4096]{2,1,0:T(8,128)(2,1)}, u32[]{:S(2)}) copy-start(bf16[1,256,4096]{2,1,0:T(8,128)(2,1)} %param.9) | copy-start | bytes 6291460
  10.9 46.3 %slice-start = ((s8[7340032]{0:T(1024)(128)(4,1)}), s8[4194304]{0:T(1024)(128)(4,1)S(1)}, s32[]{:S(2)}) async-start(s8[7340032]{0:T(1024)(128)(4,1)} %bitcast.145), calls=%async_computation | async-start | bytes 8388608
  11.6 45.6 %slice-start.1 = ((s8[7340032]{0:T(1024)(128)(4,1)}), s8[3145728]{0:T(1024)(128)(4,1)S(1)}, s32[]{:S(2)}) async-start(s8[7340032]{0:T(1024)(128)(4,1)} %bitcast.145), calls=%async_computation.1 | async-start | bytes 6291456
  56.4 101.9 %copy-start.4 = (bf16[1,256,4096]{2,1,0:T(8,128)(2,1)}, bf16[1,256,4096]{2,1,0:T(8,128)(2,1)S(1)}, u32[]{:S(2)}) copy-start(bf16[1,256,4096]{2,1,0:T(8,128)(2,1)S(1)} %get-tuple-element.13) | copy-start | bytes 6291460
  56.4 3.2 %slice-start.2 = ((s8[7340032]{0:T(1024)(128)(4,1)}), s8[4194304]{0:T(1024)(128)(4,1)S(1)}, s32[]{:S(2)}) async-start(s8[7340032]{0:T(1024)(128)(4,1)} %bitcast.147), calls=%async_computation.2 | async-start | bytes 8388608
  57.2 2.9 %copy-start.8 = (bf16[1,256,4096]{2,1,0:T(8,128)(2,1)S(1)}, bf16[1,256,4096]{2,1,0:T(8,128)(2,1)}, u32[]{:S(2)}) copy-start(bf16[1,256,4096]{2,1,0:T(8,128)(2,1)} %param.17) | copy-start | bytes 6291460
  57.2 3.8 %slice-start.3 = ((s8[7340032]{0:T(1024)(128)(4,1)}), s8[3145728]{0:T(1024)(128)(4,1)S(1)}, s32[]{:S(2)}) async-start(s8[7340032]{0:T(1024)(128)(4,1)} %bitcast.147), calls=%async_computation.3 | async-start | bytes 6291456
  63.8 2.4 copy-start.14
  160.7 1.3 copy-start.6
  178.6 40.8 %copy-start.3 = (bf16[1,256,4096]{2,1,0:T(8,128)(2,1)S(1)}, bf16[1,256,4096]{2,1,0:T(8,128)(2,1)}, u32[]{:S(2)}) copy-start(bf16[1,256,4096]{2,1,0:T(8,128)(2,1)} %param.9) | copy-start | bytes 6291460
  219.4 3.6 %copy-start.7 = (bf16[1,256,4096]{2,1,0:T(8,128)(2,1)S(1)}, bf16[1,256,4096]{2,1,0:T(8,128)(2,1)}, u32[]{:S(2)}) copy-start(bf16[1,256,4096]{2,1,0:T(8,128)(2,1)} %copy-done.6) | copy-start | bytes 6291460
  223.0 3.8 %copy-start.5 = (bf16[1,256,4096]{2,1,0:T(8,128)(2,1)S(1)}, bf16[1,256,4096]{2,1,0:T(8,128)(2,1)}, u32[]{:S(2)}) copy-start(bf16[1,256,4096]{2,1,0:T(8,128)(2,1)} %copy-done.4) | copy-start | bytes 6291460
  223.0 3.8 %copy-start.15 = (bf16[256,896]{1,0:T(8,128)(2,1)S(1)}, bf16[256,896]{1,0:T(8,128)(2,1)}, u32[]{:S(2)}) copy-start(bf16[256,896]{1,0:T(8,128)(2,1)} %copy-done.14) | copy-start | bytes 1376260
  232.6 4.9 %copy-start.9 = (bf16[1,256,4096]{2,1,0:T(8,128)(2,1)S(1)}, bf16[1,256,4096]{2,1,0:T(8,128)(2,1)}, u32[]{:S(2)}) copy-start(bf16[1,256,4096]{2,1,0:T(8,128)(2,1)} %param.17) | copy-start | bytes 6291460

commit v2 on v0

v2 whole, which is shorter than its diff:
```python
import jax
import jax.numpy as jnp
from jax import lax
from jax.experimental import pallas as pl
from jax.experimental.pallas import tpu as pltpu
from jax.sharding import PartitionSpec as P

LN_EPS = 1e-5
MESH = pl.DeviceIdType.MESH
BF16 = jnp.bfloat16
F32 = jnp.float32
WIDTH = 4096
CHUNK = 512
CHUNKS = WIDTH // CHUNK
SCALE = 128 ** -0.5
GELU_A = 0.7978845608028654
GELU_B = 0.044715


def flip(z, k):
    return (z // 2 + k // 2) % 2 * 2 + (z % 2 + k % 2) % 2


def dot_nn(a, b):
    return jnp.dot(a, b, preferred_element_type=F32)


def dot_nt(a, b):
    return lax.dot_general(a, b, (((1,), (1,)), ((), ())), preferred_element_type=F32)


def span(j):
    return pl.ds(j * CHUNK, CHUNK)


def fold(v):
    return sum(v[..., i * 128:(i + 1) * 128] for i in range(CHUNK // 128))


def row_stats(wide):
    total = sum(fold(wide(j)) for j in range(CHUNKS))
    mean = jnp.sum(total, axis=-1, keepdims=True) / WIDTH

    def square(j):
        centered = wide(j) - mean
        return fold(centered * centered)
    total = sum(square(j) for j in range(CHUNKS))
    var = jnp.sum(total, axis=-1, keepdims=True) / WIDTH
    return mean, lax.rsqrt(var + LN_EPS)


class Place:
    def __init__(self):
        me = lax.axis_index('model')
        self.core, self.y, self.z = me % 2, me // 2 % 2, me // 4
        self.partner = self.device(self.z, self.y, 1 - self.core)
        self.y_peer = self.device(self.z, 1 - self.y, self.core)
        self.z_peers = [None] + [self.device(flip(self.z, k), self.y, self.core) for k in (1, 2, 3)]
        self.own = self.block(self.core, self.y, self.z)

    def device(self, z, y, c):
        return {'model': (z * 2 + y) * 2 + c}

    def block(self, c, y, z):
        return c * 8 + y * 4 + z


def remote(src, dst, sems, dev):
    cp = pltpu.make_async_remote_copy(src_ref=src, dst_ref=dst, send_sem=sems[0], recv_sem=sems[1], device_id=dev, device_id_type=MESH)
    cp.start()
    return cp


class ReduceScatter:
    def __init__(self, place, part, bufs, sems):
        self.place, self.part = place, part
        self.buf_core, self.out_y, self.buf_y, self.sum_z, self.buf_z = bufs
        self.sems = sems
        self.core_copies, self.y_copies, self.z_copies = {}, {}, {}

    def sem(self, i):
        return self.sems.at[0, i], self.sems.at[1, i]

    def start(self):
        p = self.place
        for k in (3, 2, 1, 0):
            for j in (1, 0):
                b = p.block(1 - p.core, (p.y + j) % 2, flip(p.z, k))
                self.core_copies[k, j] = remote(self.part.at[b], self.buf_core.at[k, j], self.sem(k * 2 + j), p.partner)

    def core_step(self, k):
        p = self.place
        self.core_copies[k, 1].wait_recv()
        b = p.block(p.core, 1 - p.y, flip(p.z, k))
        for j in range(CHUNKS):
            c = span(j)
            self.out_y[k, :, c] = (self.part[b, :, c].astype(F32) + self.buf_core[k, 1, :, c].astype(F32)).astype(BF16)
        self.y_copies[k] = remote(self.out_y.at[k], self.buf_y.at[k], self.sem(8 + k), p.y_peer)

    def chip_sum(self, k, b, c):
        return self.part[b, :, c].astype(F32) + self.buf_core[k, 0, :, c].astype(F32) + self.buf_y[k, :, c].astype(F32)

    def y_step(self, k):
        p = self.place
        self.core_copies[k, 0].wait_recv()
        self.y_copies[k].wait_recv()
        b = p.block(p.core, p.y, flip(p.z, k))
        for j in range(CHUNKS):
            c = span(j)
            self.sum_z[k - 1, :, c] = self.chip_sum(k, b, c).astype(BF16)
        self.z_copies[k] = remote(self.sum_z.at[k - 1], self.buf_z.at[k - 1], self.sem(12 + k), p.z_peers[k])

    def finish(self):
        self.core_copies[0, 0].wait_recv()
        self.y_copies[0].wait_recv()
        for k in (3, 2, 1):
            self.z_copies[k].wait_recv()

    def total(self, c):
        t = self.chip_sum(0, self.place.own, c)
        for k in (3, 2, 1):
            t = t + self.buf_z[k - 1, :, c].astype(F32)
        return t

    def drain(self):
        for group in (self.core_copies, self.y_copies, self.z_copies):
            for cp in group.values():
                cp.wait_send()


class Gather:
    def __init__(self, place, full, sems):
        self.place, self.full, self.sems = place, full, sems
        self.z_out, self.y_out, self.c_out, self.sent = {}, {}, {}, []

    def send(self, b, i, dev):
        cp = remote(self.full.at[b], self.full.at[b], (self.sems.at[0, i], self.sems.at[1, i]), dev)
        self.sent.append(cp)
        return cp

    def start(self):
        p = self.place
        for k in (3, 2, 1):
            self.z_out[k] = self.send(p.own, k, p.z_peers[k])
        self.y_out[0] = self.send(p.own, 4, p.y_peer)
        self.c_out[0, 0] = self.send(p.own, 8, p.partner)

    def z_step(self, k):
        p = self.place
        self.z_out[k].wait_recv()
        b = p.block(p.core, p.y, flip(p.z, k))
        self.y_out[k] = self.send(b, 4 + k, p.y_peer)
        self.c_out[0, k] = self.send(b, 8 + k, p.partner)

    def y_step(self, k):
        p = self.place
        self.y_out[k].wait_recv()
        self.c_out[1, k] = self.send(p.block(p.core, 1 - p.y, flip(p.z, k)), 12 + k, p.partner)

    def finish(self):
        for cp in self.c_out.values():
            cp.wait_recv()

    def drain(self):
        for cp in self.sent:
            cp.wait_send()


def layer_kernel(
    x_hbm, dy_hbm, g1, g2, seg_row, seg_col, wqkv_hbm, wo_hbm, w1_hbm, w2_hbm,
    y_hbm, dx_hbm, dg_out, a_hbm, dqkv_hbm, o_hbm, dr_hbm, b1_hbm, du_hbm, gelu_hbm,
    x, dy, wqkv, wo, w1, w2, a, f1, f2, fy, fx, part1, part3, part_y,
    core_buf, yout_buf, y_buf, zsum_buf, z_buf,
    qkv, prob, o, up, gelu, d_gelu, d_up, d_attn, dqkv, x1, d_res, wide, dg_part, dg_core, dg_y, dg_sum, dg_z, dg_full,
    rs_sems, ag_sems, dg_sems, in_sems, out_sems,
):
    place = Place()
    own = place.own

    loads = [
        pltpu.make_async_copy(src, dst, in_sems.at[i])
        for i, (src, dst) in enumerate([(x_hbm, x), (wqkv_hbm, wqkv), (wo_hbm, wo), (dy_hbm, dy), (w2_hbm, w2), (w1_hbm, w1)])
    ]
    load_x, load_wqkv, load_wo, load_dy, load_w2, load_w1 = loads
    load_x.start()
    load_wqkv.start()
    stores = []

    def store(src, dst):
        cp = pltpu.make_async_copy(src, dst, out_sems.at[len(stores)])
        cp.start()
        stores.append(cp)

    barrier = pltpu.get_barrier_semaphore()
    for dev in [place.partner, place.y_peer] + place.z_peers[1:]:
        pl.semaphore_signal(barrier, inc=1, device_id=dev, device_id_type=MESH)

    def rs_set(i, part):
        bufs = [ref.at[i] for ref in (core_buf, yout_buf, y_buf, zsum_buf, z_buf)]
        return ReduceScatter(place, part, bufs, rs_sems.at[i])

    rs1, rs3, rsy, rs4 = rs_set(0, part1), rs_set(1, part3), rs_set(2, part_y), rs_set(3, part1)
    ag1, ag3, agy, ag4 = [Gather(place, ref, ag_sems.at[i]) for i, ref in enumerate((f1, f2, fy, fx))]

    def gain(ref, j):
        return ref[:, span(j)].astype(F32)

    load_x.wait()
    for cp in (load_wo, load_dy, load_w2, load_w1):
        cp.start()

    def ln_one(i, carry):
        rows = pl.ds(i * 2, 2)
        mean, rstd = row_stats(lambda j: x[rows, :, span(j)].astype(F32))
        for j in range(CHUNKS):
            c = span(j)
            normed = (x[rows, :, c].astype(F32) - mean) * rstd * gain(g1, j)[None]
            a[rows, :, c] = normed.astype(BF16)
        return carry
    lax.fori_loop(0, 8, ln_one, 0)
    store(a, a_hbm)

    load_wqkv.wait()
    qkv[...] = dot_nn(a[...].reshape(256, WIDTH), wqkv[...]).astype(BF16)

    q_pos = lax.broadcasted_iota(jnp.int32, (256, 256), 0)
    k_pos = lax.broadcasted_iota(jnp.int32, (256, 256), 1)
    allowed = (q_pos >= k_pos) & (seg_col[...] == seg_row[...])
    for h in range(2):
        q, k, v = [qkv[:, pl.ds(h * 384 + i * 128, 128)] for i in range(3)]
        scores = jnp.where(allowed, dot_nt(q, k) * SCALE, -1e30)
        exp_scores = jnp.exp(scores - jnp.max(scores, axis=-1, keepdims=True))
        p = exp_scores / jnp.sum(exp_scores, axis=-1, keepdims=True)
        prob[h] = p
        o[:, pl.ds(h * 128, 128)] = dot_nn(p.astype(BF16), v).astype(BF16)

    def project(lhs, weight, part, tile, transposed, lo=0, hi=WIDTH):
        def step(i, carry):
            c = pl.ds(pl.multiple_of(lo + i * tile, tile), tile)
            r = dot_nt(lhs[...], weight[c, :]) if transposed else dot_nn(lhs[...], weight[:, c])
            part[:, :, c] = r.astype(BF16).reshape(16, 16, tile)
            return carry
        lax.fori_loop(0, (hi - lo) // tile, step, 0)

    load_wo.wait()
    project(o, wo, part1, 512, False)
    store(o, o_hbm)
    pl.semaphore_wait(barrier, 5)

    rs1.start()
    for k in (3, 2, 1, 0):
        rs1.core_step(k)

    def d_gelu_tile(lo, n):
        c = pl.ds(lo, n)
        d_gelu[:, c] = dot_nt(dy[...].reshape(256, WIDTH), w2[c, :]).astype(BF16)
    load_dy.wait()
    load_w2.wait()
    d_gelu_tile(0, 256)
    rs1.y_step(3)
    d_gelu_tile(256, 256)
    rs1.y_step(2)
    d_gelu_tile(512, 256)
    rs1.y_step(1)
    d_gelu_tile(768, 128)
    rs1.finish()

    for j in range(CHUNKS):
        c = span(j)
        x1[:, c] = (x[own, :, c].astype(F32) + rs1.total(c)).astype(BF16)
    mean2, rstd2 = row_stats(lambda j: x1[:, span(j)].astype(F32))
    for j in range(CHUNKS):
        c = span(j)
        f1[own, :, c] = ((x1[:, c].astype(F32) - mean2) * rstd2 * gain(g2, j)).astype(BF16)
    ag1.start()
    for k in (1, 2, 3):
        ag1.z_step(k)
    for k in (0, 1, 2, 3):
        ag1.y_step(k)
    load_w1.wait()
    ag1.finish()
    store(f1, b1_hbm)

    for lo, n in ((0, 512), (512, 384)):
        c = pl.ds(lo, n)
        up[:, c] = dot_nn(f1[...].reshape(256, WIDTH), w1[:, c]).astype(BF16)

    def activation(i, carry):
        rows = pl.ds(pl.multiple_of(i * 16, 16), 16)
        u = up[rows, :].astype(F32)
        t = jnp.tanh(GELU_A * (u + GELU_B * (u * u * u)))
        gelu[rows, :] = (0.5 * u * (1.0 + t)).astype(BF16)
        slope = 0.5 * (1.0 + t) + 0.5 * u * (1.0 - t * t) * (GELU_A * (1.0 + 3.0 * GELU_B * (u * u)))
        d_up[rows, :] = (d_gelu[rows, :].astype(F32) * slope).astype(BF16)
        return carry
    lax.fori_loop(0, 16, activation, 0)
    store(gelu, gelu_hbm)
    store(d_up, du_hbm)
    project(d_up, w1, part3, 1024, True)

    rs3.start()
    for k in (3, 2, 1, 0):
        rs3.core_step(k)
    project(gelu, w2, part_y, 1024, False, 0, 2048)
    rs3.y_step(3)
    project(gelu, w2, part_y, 1024, False, 2048, 4096)
    rsy.start()
    rs3.y_step(2)
    rsy.core_step(3)
    rs3.y_step(1)
    rsy.core_step(2)
    rs3.finish()

    def ln_backward(rs, z, mean, rstd, gain_ref, dg_row):
        sum_a = jnp.zeros((16, 128), F32)
        sum_b = jnp.zeros((16, 128), F32)
        for j in range(CHUNKS):
            d_norm = rs.total(span(j)).astype(BF16).astype(F32)
            x_hat = (z(j) - mean) * rstd
            grad_row = jnp.sum(d_norm * x_hat, axis=0, keepdims=True)
            for i in range(CHUNK // 128):
                at = j * (CHUNK // 128) + i
                dg_part[at // 2, pl.ds(dg_row + at % 2, 1), :] = grad_row[:, i * 128:(i + 1) * 128]
            scaled = d_norm * gain(gain_ref, j)
            wide[:, span(j)] = scaled
            sum_a = sum_a + fold(scaled)
            sum_b = sum_b + fold(scaled * x_hat)
        mean_a = jnp.sum(sum_a, axis=-1, keepdims=True) / WIDTH
        mean_b = jnp.sum(sum_b, axis=-1, keepdims=True) / WIDTH
        for j in range(CHUNKS):
            c = span(j)
            x_hat = (z(j) - mean) * rstd
            wide[:, c] = rstd * (wide[:, c] - mean_a - x_hat * mean_b)

    ln_backward(rs3, lambda j: x1[:, span(j)].astype(F32), mean2, rstd2, g2, 2)
    for j in range(CHUNKS):
        c = span(j)
        value = (dy[own, :, c].astype(F32) + wide[:, c].astype(BF16).astype(F32)).astype(BF16)
        d_res[:, c] = value
        f2[own, :, c] = value
    ag3.start()
    for k in (1, 2, 3):
        ag3.z_step(k)
    rsy.core_step(1)
    rsy.core_step(0)
    for k in (0, 1, 2, 3):
        ag3.y_step(k)
    rsy.y_step(3)
    rsy.y_step(2)
    ag3.finish()
    store(f2, dr_hbm)

    d_attn[...] = dot_nt(f2[...].reshape(256, WIDTH), wo[...]).astype(BF16)
    for h in range(2):
        q, k, v = [qkv[:, pl.ds(h * 384 + i * 128, 128)] for i in range(3)]
        d_o = d_attn[:, pl.ds(h * 128, 128)]
        p = prob[h]
        d_prob = dot_nt(d_o, v)
        d_score = p * (d_prob - jnp.sum(p * d_prob, axis=-1, keepdims=True)) * SCALE
        dqkv[:, pl.ds(h * 384, 128)] = dot_nn(d_score.astype(BF16), k).astype(BF16)
        dqkv[:, pl.ds(h * 384 + 128, 128)] = dot_nn(d_score.T.astype(BF16), q).astype(BF16)
        dqkv[:, pl.ds(h * 384 + 256, 128)] = dot_nn(p.T.astype(BF16), d_o).astype(BF16)
    store(dqkv, dqkv_hbm)
    rs1.drain()
    project(dqkv, wqkv, part1, 1024, True)

    rs4.start()
    for k in (3, 2, 1, 0):
        rs4.core_step(k)
    rsy.y_step(1)
    rsy.finish()
    for j in range(CHUNKS):
        c = span(j)
        fy[own, :, c] = (x1[:, c].astype(F32) + rsy.total(c)).astype(BF16)
    agy.start()
    rs4.y_step(3)
    rs4.y_step(2)
    agy.z_step(1)
    rs4.y_step(1)
    agy.z_step(2)
    agy.z_step(3)
    rs4.finish()

    mean1, rstd1 = row_stats(lambda j: x[own, :, span(j)].astype(F32))
    ln_backward(rs4, lambda j: x[own, :, span(j)].astype(F32), mean1, rstd1, g1, 0)
    for j in range(CHUNKS):
        c = span(j)
        fx[own, :, c] = (d_res[:, c].astype(F32) + wide[:, c].astype(BF16).astype(F32)).astype(BF16)
    ag4.start()

    def dg_sem(i):
        return dg_sems.at[0, i], dg_sems.at[1, i]
    dg_copies = []

    def dg_send(src, dst, i, dev):
        cp = remote(src, dst, dg_sem(i), dev)
        dg_copies.append(cp)
        return cp
    half = pl.ds((1 - place.core) * 8, 8)
    dg_send(dg_part.at[half], dg_core, 0, place.partner).wait_recv()
    dg_core[...] = dg_core[...] + dg_part[pl.ds(place.core * 8, 8)]
    dg_send(dg_core.at[pl.ds((1 - place.y) * 4, 4)], dg_y, 1, place.y_peer).wait_recv()
    dg_sum[...] = dg_core[pl.ds(place.y * 4, 4)] + dg_y[...]
    arrivals = [dg_send(dg_sum.at[flip(place.z, k)], dg_z.at[k - 1], 1 + k, place.z_peers[k]) for k in (1, 2, 3)]
    for k in (1, 2, 3):
        ag4.z_step(k)
    for cp in arrivals:
        cp.wait_recv()
    dg_full[own] = dg_sum[place.z] + dg_z[0] + dg_z[1] + dg_z[2]
    arrivals = [dg_send(dg_full.at[own], dg_full.at[own], 4 + k, place.z_peers[k]) for k in (1, 2, 3)]
    for k in (0, 1, 2, 3):
        agy.y_step(k)
    for k in (0, 1):
        ag4.y_step(k)
    for cp in arrivals:
        cp.wait_recv()
    quarter = pl.ds(place.core * 8 + place.y * 4, 4)
    cp = dg_send(dg_full.at[quarter], dg_full.at[quarter], 8, place.y_peer)
    ag4.y_step(2)
    cp.wait_recv()
    mine = pl.ds(place.core * 8, 8)
    cp = dg_send(dg_full.at[mine], dg_full.at[mine], 9, place.partner)
    ag4.y_step(3)
    agy.finish()
    store(fy, y_hbm)
    cp.wait_recv()
    dg_out[...] = dg_full[...].astype(BF16)
    ag4.finish()
    store(fx, dx_hbm)

    for rs in (rs3, rsy, rs4):
        rs.drain()
    for ag in (ag1, ag3, agy, ag4):
        ag.drain()
    for cp in dg_copies:
        cp.wait_send()
    for cp in stores:
        cp.wait()


def layer(x_in, d_y, gain_one, gain_two, seg_ids, w_qkv, w_out, w_up, w_down):
    hbm = pl.BlockSpec(memory_space=pl.ANY)
    vmem = pl.BlockSpec(memory_space=pltpu.VMEM)
    dma = pltpu.SemaphoreType.DMA

    def shape(*dims, dtype=BF16):
        return jax.ShapeDtypeStruct(dims, dtype)
    blocks = (16, 16, WIDTH)
    return pl.pallas_call(
        layer_kernel,
        out_shape=[
            shape(*blocks), shape(*blocks), shape(16, 4, 128), shape(*blocks), shape(256, 768), shape(256, 256), shape(*blocks),
            shape(*blocks), shape(256, 896), shape(256, 896),
        ],
        in_specs=[hbm, hbm, vmem, vmem, vmem, vmem, hbm, hbm, hbm, hbm],
        out_specs=[hbm, hbm, vmem] + [hbm] * 7,
        scratch_shapes=[
            pltpu.VMEM(blocks, BF16), pltpu.VMEM(blocks, BF16),
            pltpu.VMEM((WIDTH, 768), BF16), pltpu.VMEM((256, WIDTH), BF16), pltpu.VMEM((WIDTH, 896), BF16), pltpu.VMEM((896, WIDTH), BF16),
        ] + [pltpu.VMEM(blocks, BF16)] * 8 + [
            pltpu.VMEM((4, 4, 2, 16, WIDTH), BF16), pltpu.VMEM((4, 4, 16, WIDTH), BF16), pltpu.VMEM((4, 4, 16, WIDTH), BF16),
            pltpu.VMEM((4, 3, 16, WIDTH), BF16), pltpu.VMEM((4, 3, 16, WIDTH), BF16),
            pltpu.VMEM((256, 768), BF16), pltpu.VMEM((2, 256, 256), F32), pltpu.VMEM((256, 256), BF16),
        ] + [pltpu.VMEM((256, 896), BF16)] * 4 + [
            pltpu.VMEM((256, 256), BF16), pltpu.VMEM((256, 768), BF16), pltpu.VMEM((16, WIDTH), BF16), pltpu.VMEM((16, WIDTH), BF16),
            pltpu.VMEM((16, WIDTH), F32),
            pltpu.VMEM((16, 4, 128), F32), pltpu.VMEM((8, 4, 128), F32), pltpu.VMEM((4, 4, 128), F32), pltpu.VMEM((4, 4, 128), F32),
            pltpu.VMEM((3, 4, 128), F32), pltpu.VMEM((16, 4, 128), F32),
            dma((4, 2, 16)), dma((4, 2, 16)), dma((2, 10)), dma((6,)), dma((9,)),
        ],
        compiler_params=pltpu.CompilerParams(collective_id=0, has_side_effects=True, vmem_limit_bytes=66 * 10 ** 6),
        name='layer',
    )(
        x_in.reshape(blocks), d_y.reshape(blocks), gain_one.reshape(1, WIDTH), gain_two.reshape(1, WIDTH), seg_ids.reshape(1, 256), seg_ids.reshape(256, 1),
        w_qkv, w_out.reshape(256, WIDTH), w_up, w_down,
    )


def solution(mesh):
    def local_step(x_in, seg_ids, gain_one, w_qkv, w_out, gain_two, w_up, w_down, d_y):
        y_out, d_x, d_gains, normed_one, d_qkv, attn_out, d_resid, normed_two, d_up, gelu_out = layer(x_in, d_y, gain_one, gain_two, seg_ids, w_qkv, w_out, w_up, w_down)

        def weight_grad(a, b):
            return lax.dot_general(a.reshape(256, -1), b.reshape(256, -1), (((0,), (0,)), ((), ())), preferred_element_type=F32).astype(BF16)
        d_w_qkv = weight_grad(normed_one, d_qkv)
        d_w_out = weight_grad(attn_out, d_resid).reshape(w_out.shape)
        d_w_up = weight_grad(normed_two, d_up)
        d_w_down = weight_grad(gelu_out, d_y)
        d_gain_one = d_gains[:, 0:2].reshape(WIDTH)
        d_gain_two = d_gains[:, 2:4].reshape(WIDTH)
        return y_out.reshape(x_in.shape), d_x.reshape(x_in.shape), d_w_qkv, d_w_out, d_w_up, d_w_down, d_gain_one, d_gain_two

    in_specs = (P('data'), P('data'), P(), P(None, 'model'), P('model'), P(), P(None, 'model'), P('model'), P('data'))
    out_specs = (P('data'), P('data'), P('data', 'model'), P(('data', 'model')), P('data', 'model'), P(('data', 'model')), P('data'), P('data'))
    return jax.shard_map(local_step, mesh=mesh, in_specs=in_specs, out_specs=out_specs, check_vma=False)
```

time: 395 us -> 181 us (0.46)
  waiting for transfers between devices: 280 us -> 0 us
  Pallas kernels: 0 us -> 152 us
  matrix products: 60.4 us -> 19 us
  other arithmetic: 31.3 us -> 0 us
  between operations: 14.2 us -> 0.67 us
  local copies, waits for them, and re-layouts: 4.24 us -> 9.2 us
    psum x3 -> x0, waiting for transfers between devices: 280 us -> none  [the longest x1 100 us: local_step(): sum_one = lax.psum(part_one, 'model')]
    pallas_call x0 -> x1, Pallas kernels: none -> 152 us  [layer(): pl.pallas_call(layer_kernel, out_shape=[shape(*blocks), shape(*blocks), s...]
    dot_general x18 -> x4, matrix products: 60.4 us -> 19 us  [weight_grad(): lax.dot_general(a.reshape(256, -1), b.reshape(256, -1), (((0,), (0,)), ((...]
    reduce_sum x9 -> x0, other arithmetic: 23.8 us -> none  [the longest x4 15.6 us: layer_norm(): centered * lax.rsqrt(row_var + LN_EPS) * gain.astype(jnp.float32)]
    add x3 -> x0, other arithmetic: 6.24 us -> none  [the longest x1 3.75 us: local_step(): d_x = d_resid + d_x_ln]
    reshape x0 -> x3, local copies, waits for them, and re-layouts: none -> 4.1 us  [the longest x1 1.47 us: layer(): seg_ids.reshape(256, 1)]
  transfers between devices with their start and end apart: 3 -> 0, of which waited for: 3 -> 0; matrix products, arithmetic and copies ran while one was open for 7% -> 0% of each run, Pallas kernels for 0% -> 0%
where the time goes in v2:
time: 181 us
  Pallas kernels  152 us (84%)
  matrix products  19 us (10%)
  local copies, waits for them, and re-layouts  9.2 us (5%)
    pallas_call x1, Pallas kernels, layer(): pl.pallas_call(layer_kernel, out_shape=[shape(*blocks), shape(*blocks), s...  152 us
    dot_general x4, matrix products, weight_grad(): lax.dot_general(a.reshape(256, -1), b.reshape(256, -1), (((0,), (0,)), ((...  19 us
    unnamed x18, local copies, waits for them, and re-layouts  3.69 us

profile of v2, /device:TPU:0, one launch (start us, length us, event | category | flops | bytes accessed | tf_op | source)
XLA Modules:
  0.0 180.5 jit_solution(13118475623719320450)
XLA Ops:
  0.6 1.3 reshape.63.g1
  1.9 1.3 reshape.64.g2
  3.3 1.5 copy.17.seg_col
  4.7 151.6 %layer.1 = (bf16[16,16,4096]{2,1,0:T(8,128)(2,1)}, bf16[16,16,4096]{2,1,0:T(8,128)(2,1)}, bf16[16,4,128]{2,1,0:T(4,128)(2,1)}, bf16[16,16,4096]{2,1,0:T(8,128)(2...) custom-call(bf16[16,16,4096]{2,1,0:T(8,128)(2,1)} %bitcast.29, ...), custom_call_target="tpu_custom_call" | custom-call | tf_op jit(solution)/shard_map/layer/pallas_call | solution.py:449
  156.4 1.4 fusion.1
  157.8 0.0 copy-start.1
  157.8 0.0 copy-start.7
  157.8 3.9 %convolution_convert_fusion.3 = bf16[256,4096]{1,0:T(8,128)(2,1)} fusion(bf16[256,256]{1,0:T(8,128)(2,1)} %get-tuple-element.22, bf16[256,4096]{1,0:T(8,128)(2,1)} %bitcast.28), kind=kOutput, calls=%fused_computation.3 | convolution fusion | flops 537919488 | bytes 4325376 | tf_op jit(solution)/shard_map/dot_general | solution.py:484
  161.6 0.0 copy-done.1
  161.6 0.0 copy-done.7
  161.6 0.0 copy-start.2
  161.6 0.0 copy-start.6
  161.6 4.6 %convolution_convert_fusion.2 = bf16[4096,768]{1,0:T(8,128)(2,1)} fusion(bf16[256,4096]{1,0:T(8,128)(2,1)S(1)} %bitcast.23, bf16[256,768]{1,0:T(8,128)(2,1)S(1)} %copy-done.7), kind=kOutput, calls=%fused_computation.2 | convolution fusion | flops 1613758464 | bytes 8781824 | tf_op jit(solution)/shard_map/dot_general | solution.py:484
  166.2 0.0 copy-done.2
  166.2 0.0 copy-done.6
  166.2 0.0 copy-start
  166.2 5.4 %convolution_convert_fusion.1 = bf16[4096,896]{1,0:T(8,128)(2,1)} fusion(bf16[256,4096]{1,0:T(8,128)(2,1)S(1)} %bitcast.24, bf16[256,896]{1,0:T(8,128)(2,1)S(1)} %copy-done.6), kind=kOutput, calls=%fused_computation.1 | convolution fusion | flops 1882718208 | bytes 9895936 | tf_op jit(solution)/shard_map/dot_general | solution.py:484
  171.7 0.0 copy-done
  171.7 0.0 copy-done.5
  171.7 5.2 %convolution_convert_fusion = bf16[896,4096]{1,0:T(8,128)(2,1)} fusion(bf16[256,896]{1,0:T(8,128)(2,1)S(1)} %copy-done.5, bf16[1,256,4096]{2,1,0:T(8,128)(2,1)S(1)} %copy-done), kind=kOutput, calls=%fused_computation | convolution fusion | flops 1882718208 | bytes 9895936 | tf_op jit(solution)/shard_map/dot_general | solution.py:484
  176.8 0.0 copy-done.4
  176.8 1.3 copy.20
  178.2 1.0 copy-done.3
  179.2 1.3 copy.21
  (3 shorter events, 0.0 us)
Async XLA Ops:
  157.8 3.9 %copy-start.1 = (bf16[16,16,4096]{2,1,0:T(8,128)(2,1)S(1)}, bf16[16,16,4096]{2,1,0:T(8,128)(2,1)}, u32[]{:S(2)}) copy-start(bf16[16,16,4096]{2,1,0:T(8,128)(2,1)} %get-tuple-element.20) | copy-start | bytes 6291460
  157.8 3.9 %copy-start.7 = (bf16[256,768]{1,0:T(8,128)(2,1)S(1)}, bf16[256,768]{1,0:T(8,128)(2,1)}, u32[]{:S(2)}) copy-start(bf16[256,768]{1,0:T(8,128)(2,1)} %get-tuple-element.21) | copy-start | bytes 1179652
  161.6 4.6 %copy-start.2 = (bf16[16,16,4096]{2,1,0:T(8,128)(2,1)S(1)}, bf16[16,16,4096]{2,1,0:T(8,128)(2,1)}, u32[]{:S(2)}) copy-start(bf16[16,16,4096]{2,1,0:T(8,128)(2,1)} %get-tuple-element.24) | copy-start | bytes 6291460
  161.6 4.6 %copy-start.6 = (bf16[256,896]{1,0:T(8,128)(2,1)S(1)}, bf16[256,896]{1,0:T(8,128)(2,1)}, u32[]{:S(2)}) copy-start(bf16[256,896]{1,0:T(8,128)(2,1)} %get-tuple-element.25) | copy-start | bytes 1376260
  166.2 5.4 %copy-start = (bf16[1,256,4096]{2,1,0:T(8,128)(2,1)S(1)}, bf16[1,256,4096]{2,1,0:T(8,128)(2,1)}, u32[]{:S(2)}) copy-start(bf16[1,256,4096]{2,1,0:T(8,128)(2,1)} %param.17) | copy-start | bytes 6291460
  166.2 5.4 %copy-start.5 = (bf16[256,896]{1,0:T(8,128)(2,1)S(1)}, bf16[256,896]{1,0:T(8,128)(2,1)}, u32[]{:S(2)}) copy-start(bf16[256,896]{1,0:T(8,128)(2,1)} %get-tuple-element.26) | copy-start | bytes 1376260
  171.7 5.2 %copy-start.4 = (bf16[16,16,4096]{2,1,0:T(8,128)(2,1)S(1)}, bf16[16,16,4096]{2,1,0:T(8,128)(2,1)}, u32[]{:S(2)}) copy-start(bf16[16,16,4096]{2,1,0:T(8,128)(2,1)} %get-tuple-element.18) | copy-start | bytes 6291460
  176.8 2.3 %copy-start.3 = (bf16[16,16,4096]{2,1,0:T(8,128)(2,1)S(1)}, bf16[16,16,4096]{2,1,0:T(8,128)(2,1)}, u32[]{:S(2)}) copy-start(bf16[16,16,4096]{2,1,0:T(8,128)(2,1)} %get-tuple-element.19) | copy-start | bytes 6291460

commit v3 on v2

v3 whole, which is shorter than its diff:
```python
import jax
import jax.numpy as jnp
from jax import lax
from jax.experimental import pallas as pl
from jax.experimental.pallas import tpu as pltpu
from jax.sharding import PartitionSpec as P

LN_EPS = 1e-5
MESH = pl.DeviceIdType.MESH
BF16 = jnp.bfloat16
F32 = jnp.float32
WIDTH = 4096
CHUNK = 512
WO_TILE = 2048
LAYER_VMEM = 49 * 2 ** 20
GRADS_VMEM = 28 * 2 ** 20
TOKENS = 256
LANES = 128
BLOCKS = 16
FFN = 896
QKV_COLS = 768
CHUNKS = WIDTH // CHUNK
SCALE = LANES ** -0.5
GELU_A = 0.7978845608028654
GELU_B = 0.044715


def flip(z, k):
    high, low = lax.div(z, 2), lax.rem(z, 2)
    return (1 - high if k >= 2 else high) * 2 + (1 - low if k % 2 else low)


def dot_nn(a, b):
    return jnp.dot(a, b, preferred_element_type=F32)


def dot_nt(a, b):
    return lax.dot_general(a, b, (((1,), (1,)), ((), ())), preferred_element_type=F32)


def span(j):
    return pl.ds(j * CHUNK, CHUNK)


def half(h):
    return pl.ds(h * (WIDTH // 2), WIDTH // 2)


def half_spans(h):
    return [(span(h * (CHUNKS // 2) + j), span(j)) for j in range(CHUNKS // 2)]


def fold(v):
    return sum(v[..., i * LANES:(i + 1) * LANES] for i in range(CHUNK // LANES))


def row_stats(wide):
    total = sum(fold(wide(j)) for j in range(CHUNKS))
    mean = jnp.sum(total, axis=-1, keepdims=True) / WIDTH

    def square(j):
        centered = wide(j) - mean
        return fold(centered * centered)
    total = sum(square(j) for j in range(CHUNKS))
    var = jnp.sum(total, axis=-1, keepdims=True) / WIDTH
    return mean, lax.rsqrt(var + LN_EPS)


class Place:
    def __init__(self):
        me = lax.axis_index('model')
        self.core, self.y, self.z = lax.rem(me, 2), lax.rem(lax.div(me, 2), 2), lax.div(me, 4)
        self.partner = {'model': me + 1 - 2 * self.core}
        self.y_peer = {'model': me + 2 - 4 * self.y}
        self.z_at = [flip(self.z, k) for k in range(4)]
        self.z_peers = [{'model': me + (at - self.z) * 4} for at in self.z_at]
        self.blocks = {
            (i, j, k): (1 - self.core if i else self.core) * 8 + (1 - self.y if j else self.y) * 4 + self.z_at[k]
            for i in (0, 1) for j in (0, 1) for k in range(4)
        }
        self.own = self.blocks[0, 0, 0]

    def block(self, i, j, k):
        return self.blocks[i, j, k]


def remote(src, dst, sems, dev):
    cp = pltpu.make_async_remote_copy(src_ref=src, dst_ref=dst, send_sem=sems[0], recv_sem=sems[1], device_id=dev, device_id_type=MESH)
    cp.start()
    return cp


class ReduceScatter:
    def __init__(self, place, part, bufs, sems):
        self.place, self.part, self.sems = place, part, sems
        self.buf_core, self.out_y, self.buf_y, self.out_z, self.buf_z, self.out_first, self.buf_first = bufs
        self.core_in, self.y_in, self.z_in, self.first_in = {}, {}, {}, {}
        self.ready = set()

    def sem(self, i):
        return self.sems.at[0, i], self.sems.at[1, i]

    def block(self, k, j):
        return self.place.block(0, j, k)

    def start(self):
        p = self.place
        for k in (3, 1, 2, 0):
            for j in (1, 0):
                b = p.block(1, j, k)
                self.core_in[k, j] = remote(self.part.at[b], self.buf_core.at[k, j], self.sem(k * 2 + j), p.partner)

    def core_ready(self, k, j):
        if (k, j) not in self.ready:
            self.core_in[k, j].wait_recv()
            self.ready.add((k, j))

    def pair_sum(self, k, j, c):
        return self.part[self.block(k, j), :, c].astype(F32) + self.buf_core[k, j, :, c].astype(F32)

    def chip_sum(self, k, c):
        return self.pair_sum(k, 0, c) + self.buf_y[k, :, c].astype(F32)

    def send_y(self, k, h):
        self.core_ready(k, 1)
        if (k, h) == (0, 1):
            self.first_in[1].wait_recv()
        for c, d in half_spans(h):
            t = self.pair_sum(k, 1, c)
            if (k, h) == (0, 1):
                t = t + self.buf_first[1, :, d].astype(F32)
            self.out_y[k, :, c] = t.astype(BF16)
        self.y_in[k, h] = remote(self.out_y.at[k, :, half(h)], self.buf_y.at[k, :, half(h)], self.sem(8 + k * 2 + h), self.place.y_peer)

    def send_first(self):
        for j in (1, 0):
            self.core_ready(1, j)
            for c, d in half_spans(1):
                self.out_first[j, :, d] = self.pair_sum(1, j, c).astype(BF16)
            self.first_in[j] = remote(self.out_first.at[j], self.buf_first.at[j], self.sem(22 + j), self.place.z_peers[1])

    def send_z(self, k, h):
        self.core_ready(k, 0)
        self.y_in[k, h].wait_recv()
        if k == 2:
            self.z_in[3, h].wait_recv()
        for c, _ in half_spans(h):
            t = self.chip_sum(k, c)
            if k == 2:
                t = t + self.buf_z[2, :, c].astype(F32)
            self.out_z[k - 1, :, c] = t.astype(BF16)
        self.z_in[k, h] = remote(self.out_z.at[k - 1, :, half(h)], self.buf_z.at[k - 1, :, half(h)], self.sem(14 + k * 2 + h), self.place.z_peers[2 if k == 2 else 1])

    def head(self):
        return [
            lambda: self.send_y(3, 0), lambda: self.send_y(3, 1), self.send_first, lambda: self.send_y(1, 0),
            lambda: self.send_y(2, 0), lambda: self.send_y(2, 1), lambda: self.send_y(0, 0),
        ]

    def tail(self):
        return [
            lambda: self.send_z(3, 0), lambda: self.send_z(3, 1), lambda: self.send_y(0, 1),
            lambda: self.send_z(1, 0), lambda: self.send_z(2, 0), lambda: self.send_z(2, 1),
        ]

    def finish(self):
        self.core_ready(0, 0)
        self.y_in[0, 0].wait_recv()
        self.y_in[0, 1].wait_recv()
        self.first_in[0].wait_recv()
        self.z_in[1, 0].wait_recv()
        self.z_in[2, 0].wait_recv()
        self.z_in[2, 1].wait_recv()

    def total(self, j):
        c = span(j)
        near = self.buf_z[0, :, c] if j < CHUNKS // 2 else self.buf_first[0, :, span(j - CHUNKS // 2)]
        return self.chip_sum(0, c) + near.astype(F32) + self.buf_z[1, :, c].astype(F32)

    def drain(self):
        for group in (self.core_in, self.y_in, self.z_in, self.first_in):
            for cp in group.values():
                cp.wait_send()


class Gather:
    def __init__(self, place, full, sems):
        self.place, self.full, self.sems = place, full, sems
        self.z_in, self.y_in, self.core_in, self.last_in, self.sent = {}, {}, {}, {}, []

    def send(self, j, k, h, i, dev):
        b = self.place.block(0, j, k)
        ref = self.full.at[b] if h is None else self.full.at[b, :, half(h)]
        cp = remote(ref, ref, (self.sems.at[0, i], self.sems.at[1, i]), dev)
        self.sent.append(cp)
        return cp

    def to_core(self, j, k, h):
        self.core_in[j, k, h] = self.send(j, k, h, 14 + j * 8 + k * 2 + h, self.place.partner)

    def to_y(self, k, h):
        self.y_in[k, h] = self.send(0, k, h, 6 + k * 2 + h, self.place.y_peer)

    def to_z(self, k, h):
        self.z_in[k, h] = self.send(0, 2 if k == 3 else 0, h, (k - 1) * 2 + h, self.place.z_peers[2 if k == 2 else 1])

    def start_far(self):
        for h in (0, 1):
            self.to_z(2, h)

    def start_near(self):
        for h in (0, 1):
            self.to_y(0, h)
            self.to_z(1, h)
        self.core_in[0, 0, None] = self.send(0, 0, None, 30, self.place.partner)

    def from_z(self, k, h):
        self.z_in[k, h].wait_recv()
        if k == 2:
            self.to_z(3, h)
        if (k, h) != (1, 1):
            self.to_y(k, h)
        self.to_core(0, k, h)

    def from_y(self, k, h):
        self.y_in[k, h].wait_recv()
        self.to_core(1, k, h)

    def send_last(self):
        self.last_in[0] = self.send(1, 0, 1, 31, self.place.z_peers[1])

    def from_last(self):
        self.last_in[0].wait_recv()
        self.to_core(1, 1, 1)

    def steps(self):
        return [
            lambda: self.from_y(0, 0), lambda: self.from_z(2, 0), lambda: self.from_y(0, 1), lambda: self.from_z(2, 1), self.send_last,
            lambda: self.from_z(1, 0), lambda: self.from_z(1, 1), lambda: self.from_y(2, 0), lambda: self.from_y(2, 1), lambda: self.from_z(3, 0),
            lambda: self.from_y(1, 0), lambda: self.from_z(3, 1), self.from_last, lambda: self.from_y(3, 0), lambda: self.from_y(3, 1),
        ]

    def late_steps(self):
        near = [lambda: self.from_y(0, 0), lambda: self.from_y(0, 1), lambda: self.from_z(1, 0), lambda: self.from_z(1, 1)]
        far = [
            lambda: self.from_z(2, 0), lambda: self.from_z(2, 1), lambda: self.from_y(1, 0), lambda: self.from_z(3, 0), lambda: self.from_z(3, 1),
            lambda: self.from_y(2, 0), lambda: self.from_y(2, 1), self.from_last, lambda: self.from_y(3, 0), lambda: self.from_y(3, 1),
        ]
        return near, far

    def finish(self):
        for cp in self.core_in.values():
            cp.wait_recv()

    def drain(self):
        for cp in self.sent:
            cp.wait_send()


def run(steps):
    for step in steps:
        step()


def layer_kernel(
    x_hbm, dy_hbm, g1, g2, seg, wqkv_hbm, wo_hbm, w1_hbm, w2_hbm,
    fy, fx, dg1_out, dg2_out, a, dqkv, o, f2, f1, d_up, gelu, dy,
    x, wqkv, wo, w1, w2, part1, part3, part_y,
    core_buf, yout_buf, y_buf, zout_buf, z_buf, fout_buf, first_buf,
    qkv, prob, up, d_gelu, d_attn, x1, d_res, wide, dg_part, dg_core, dg_y, dg_z, dg_full,
    rs_sems, ag_sems, dg_sems, in_sems,
):
    place = Place()
    own = place.own

    loads = [
        pltpu.make_async_copy(src, dst, in_sems.at[i])
        for i, (src, dst) in enumerate([(x_hbm, x), (wqkv_hbm, wqkv), (wo_hbm, wo), (dy_hbm, dy), (w2_hbm, w2), (w1_hbm, w1)])
    ]
    load_x, load_wqkv, load_wo, load_dy, load_w2, load_w1 = loads
    load_x.start()
    load_wqkv.start()
    barrier = pltpu.get_barrier_semaphore()
    for dev in [place.partner, place.y_peer] + place.z_peers[1:]:
        pl.semaphore_signal(barrier, inc=1, device_id=dev, device_id_type=MESH)

    def rs_set(i, part):
        bufs = [ref.at[i] for ref in (core_buf, yout_buf, y_buf, zout_buf, z_buf, fout_buf, first_buf)]
        return ReduceScatter(place, part, bufs, rs_sems.at[i])

    rs1, rs3, rsy, rs4 = rs_set(0, part1), rs_set(1, part3), rs_set(2, part_y), rs_set(3, part1)
    ag1, ag3, agy, ag4 = [Gather(place, ref, ag_sems.at[i]) for i, ref in enumerate((f1, f2, fy, fx))]

    def gain(ref, j):
        return ref[span(j)].astype(F32).reshape(1, CHUNK)

    load_x.wait()
    for cp in (load_wo, load_dy, load_w2, load_w1):
        cp.start()

    def ln_one(i, carry):
        rows = pl.ds(i * 2, 2)
        mean, rstd = row_stats(lambda j: x[rows, :, span(j)].astype(F32))
        for j in range(CHUNKS):
            c = span(j)
            normed = (x[rows, :, c].astype(F32) - mean) * rstd * gain(g1, j)[None]
            a[rows, :, c] = normed.astype(BF16)
        return carry
    lax.fori_loop(0, 8, ln_one, 0)

    load_wqkv.wait()
    qkv[...] = dot_nn(a[...].reshape(TOKENS, WIDTH), wqkv[...]).astype(BF16)

    q_pos = lax.broadcasted_iota(jnp.int32, (TOKENS, TOKENS), 0)
    k_pos = lax.broadcasted_iota(jnp.int32, (TOKENS, TOKENS), 1)
    seg_keys = jnp.broadcast_to(seg[...].astype(F32), (TOKENS, TOKENS))
    allowed = (q_pos >= k_pos) & (seg_keys.T == seg_keys)
    for h in range(2):
        q, k, v = [qkv[:, pl.ds(h * 384 + i * LANES, LANES)] for i in range(3)]
        scores = jnp.where(allowed, dot_nt(q, k) * SCALE, -1e30)
        exp_scores = jnp.exp(scores - jnp.max(scores, axis=-1, keepdims=True))
        p = exp_scores / jnp.sum(exp_scores, axis=-1, keepdims=True)
        prob[h] = p
        o[:, pl.ds(h * LANES, LANES)] = dot_nn(p.astype(BF16), v).astype(BF16)

    def project(lhs, weight, part, tile, transposed, lo=0, hi=WIDTH):
        def step(i, carry):
            c = pl.ds(pl.multiple_of(lo + i * tile, tile), tile)
            r = dot_nt(lhs[...], weight[c, :]) if transposed else dot_nn(lhs[...], weight[:, c])
            part[:, :, c] = r.astype(BF16).reshape(BLOCKS, BLOCKS, tile)
            return carry
        lax.fori_loop(0, (hi - lo) // tile, step, 0)

    load_wo.wait()
    project(o, wo, part1, WO_TILE, False)
    pl.semaphore_wait(barrier, 5)

    rs1.start()
    run(rs1.head())

    def d_gelu_tile(lo, n):
        c = pl.ds(lo, n)
        d_gelu[:, c] = dot_nt(dy[...].reshape(TOKENS, WIDTH), w2[c, :]).astype(BF16)
    load_dy.wait()
    load_w2.wait()
    tail = rs1.tail()
    d_gelu_tile(0, TOKENS)
    run(tail[:4])
    d_gelu_tile(TOKENS, TOKENS)
    run(tail[4:5])
    d_gelu_tile(512, TOKENS)
    run(tail[5:])
    d_gelu_tile(QKV_COLS, LANES)
    rs1.finish()

    for j in range(CHUNKS):
        c = span(j)
        x1[:, c] = (x[own, :, c].astype(F32) + rs1.total(j)).astype(BF16)
    mean2, rstd2 = row_stats(lambda j: x1[:, span(j)].astype(F32))
    for j in range(CHUNKS):
        c = span(j)
        f1[own, :, c] = ((x1[:, c].astype(F32) - mean2) * rstd2 * gain(g2, j)).astype(BF16)
    ag1.start_far()
    ag1.start_near()
    run(ag1.steps())
    load_w1.wait()
    ag1.finish()

    for lo, n in ((0, 512), (512, 384)):
        c = pl.ds(lo, n)
        up[:, c] = dot_nn(f1[...].reshape(TOKENS, WIDTH), w1[:, c]).astype(BF16)

    def activation(i, carry):
        rows = pl.ds(pl.multiple_of(i * BLOCKS, BLOCKS), BLOCKS)
        u = up[rows, :].astype(F32)
        t = jnp.tanh(GELU_A * (u + GELU_B * (u * u * u)))
        gelu[rows, :] = (0.5 * u * (1.0 + t)).astype(BF16)
        slope = 0.5 * (1.0 + t) + 0.5 * u * (1.0 - t * t) * (GELU_A * (1.0 + 3.0 * GELU_B * (u * u)))
        d_up[rows, :] = (d_gelu[rows, :].astype(F32) * slope).astype(BF16)
        return carry
    lax.fori_loop(0, BLOCKS, activation, 0)
    project(d_up, w1, part3, WO_TILE, True)

    rs3.start()
    run(rs3.head())
    tail, y_head, y_tail = rs3.tail(), rsy.head(), rsy.tail()
    project(gelu, w2, part_y, 1024, False, 0, 2048)
    run(tail[:4])
    project(gelu, w2, part_y, 1024, False, 2048, 4096)
    rsy.start()
    run(tail[4:])
    run(y_head[:4])
    rs3.finish()

    def ln_backward(rs, z, mean, rstd, gain_ref, dg_row):
        sum_a = jnp.zeros((BLOCKS, LANES), F32)
        sum_b = jnp.zeros((BLOCKS, LANES), F32)
        for j in range(CHUNKS):
            d_norm = rs.total(j).astype(BF16).astype(F32)
            x_hat = (z(j) - mean) * rstd
            grad_row = jnp.sum(d_norm * x_hat, axis=0, keepdims=True)
            for i in range(CHUNK // LANES):
                at = j * (CHUNK // LANES) + i
                dg_part[at // 2, pl.ds(dg_row + at % 2, 1), :] = grad_row[:, i * LANES:(i + 1) * LANES]
            scaled = d_norm * gain(gain_ref, j)
            wide[:, span(j)] = scaled
            sum_a = sum_a + fold(scaled)
            sum_b = sum_b + fold(scaled * x_hat)
        mean_a = jnp.sum(sum_a, axis=-1, keepdims=True) / WIDTH
        mean_b = jnp.sum(sum_b, axis=-1, keepdims=True) / WIDTH
        for j in range(CHUNKS):
            c = span(j)
            x_hat = (z(j) - mean) * rstd
            wide[:, c] = rstd * (wide[:, c] - mean_a - x_hat * mean_b)

    ln_backward(rs3, lambda j: x1[:, span(j)].astype(F32), mean2, rstd2, g2, 2)
    for j in range(CHUNKS):
        c = span(j)
        value = (dy[own, :, c].astype(F32) + wide[:, c].astype(BF16).astype(F32)).astype(BF16)
        d_res[:, c] = value
        f2[own, :, c] = value
    ag3.start_far()
    ag3.start_near()
    steps = ag3.steps()
    run(steps[:12])
    run(y_head[4:])
    run(y_tail[:2])
    run(steps[12:])
    ag3.finish()

    d_attn[...] = dot_nt(f2[...].reshape(TOKENS, WIDTH), wo[...]).astype(BF16)
    run(y_tail[2:5])
    for h in range(2):
        q, k, v = [qkv[:, pl.ds(h * 384 + i * LANES, LANES)] for i in range(3)]
        d_o = d_attn[:, pl.ds(h * LANES, LANES)]
        p = prob[h]
        d_prob = dot_nt(d_o, v)
        d_score = p * (d_prob - jnp.sum(p * d_prob, axis=-1, keepdims=True)) * SCALE
        dqkv[:, pl.ds(h * 384, LANES)] = dot_nn(d_score.astype(BF16), k).astype(BF16)
        dqkv[:, pl.ds(h * 384 + LANES, LANES)] = dot_nn(d_score.T.astype(BF16), q).astype(BF16)
        dqkv[:, pl.ds(h * 384 + TOKENS, LANES)] = dot_nn(p.T.astype(BF16), d_o).astype(BF16)
    run(y_tail[5:])
    rs1.drain()
    project(dqkv, wqkv, part1, WO_TILE, True)

    rs4.start()
    run(rs4.head())
    rsy.finish()
    for j in range(CHUNKS):
        c = span(j)
        fy[own, :, c] = (x1[:, c].astype(F32) + rsy.total(j)).astype(BF16)
    run(rs4.tail())
    agy.start_near()
    rs4.finish()
    mean1, rstd1 = row_stats(lambda j: x[own, :, span(j)].astype(F32))
    ln_backward(rs4, lambda j: x[own, :, span(j)].astype(F32), mean1, rstd1, g1, 0)
    for j in range(CHUNKS):
        c = span(j)
        fx[own, :, c] = (d_res[:, c].astype(F32) + wide[:, c].astype(BF16).astype(F32)).astype(BF16)
    dg_copies = []

    def dg_send(src, dst, i, dev):
        cp = remote(src, dst, (dg_sems.at[0, i], dg_sems.at[1, i]), dev)
        dg_copies.append(cp)
        return cp
    in_core = dg_send(dg_part.at[pl.ds((1 - place.core) * 8, 8)], dg_core, 0, place.partner)
    ag4.start_far()
    agy.start_far()
    ag4.start_near()
    steps = ag4.steps()
    near, far = agy.late_steps()
    in_core.wait_recv()
    dg_core[...] = dg_core[...] + dg_part[pl.ds(place.core * 8, 8)]
    in_y = dg_send(dg_core.at[pl.ds((1 - place.y) * 4, 4)], dg_y, 6, place.y_peer)
    run(near)
    run(steps[:5])
    in_y.wait_recv()
    quarter = pl.ds(place.core * 8 + place.y * 4, 4)
    dg_z[place.z] = dg_core[pl.ds(place.y * 4, 4)] + dg_y[...]
    in_z = [dg_send(dg_z.at[place.z], dg_z.at[place.z], k, place.z_peers[k]) for k in (1, 2, 3)]
    run(steps[5:7])
    run(far[:2])
    agy.send_last()
    run(steps[7:10])
    run(far[2:3])
    for cp in in_z:
        cp.wait_recv()
    dg_full[quarter] = dg_z[0] + dg_z[1] + dg_z[2] + dg_z[3]
    in_y = dg_send(dg_full.at[quarter], dg_full.at[quarter], 4, place.y_peer)
    run(steps[10:13])
    run(far[3:6])
    in_y.wait_recv()
    mine = pl.ds(place.core * 8, 8)
    in_core = dg_send(dg_full.at[mine], dg_full.at[mine], 5, place.partner)
    run(steps[13:])
    in_core.wait_recv()
    for i in range(32):
        for row, out in ((0, dg1_out), (2, dg2_out)):
            out[pl.ds(i * LANES, LANES)] = dg_full[i // 2, row + i % 2].astype(BF16)
    ag4.finish()
    run(far[6:])
    agy.finish()

    for rs in (rs3, rsy, rs4):
        rs.drain()
    for ag in (ag1, ag3, agy, ag4):
        ag.drain()
    for cp in dg_copies:
        cp.wait_send()


def layer(x_in, d_y, gain_one, gain_two, seg_ids, w_qkv, w_out, w_up, w_down):
    hbm = pl.BlockSpec(memory_space=pl.ANY)
    vmem = pl.BlockSpec(memory_space=pltpu.VMEM)
    dma = pltpu.SemaphoreType.DMA

    def shape(*dims):
        return pltpu.VMEM(dims, BF16)

    def scratch(*dims, dtype=BF16):
        return pltpu.VMEM(dims, dtype)
    blocks = (BLOCKS, BLOCKS, WIDTH)
    return pl.pallas_call(
        layer_kernel,
        out_shape=[
            shape(*blocks), shape(*blocks), shape(WIDTH), shape(WIDTH), shape(*blocks), shape(TOKENS, QKV_COLS), shape(TOKENS, TOKENS), shape(*blocks),
            shape(*blocks), shape(TOKENS, FFN), shape(TOKENS, FFN), shape(*blocks),
        ],
        in_specs=[hbm, hbm, vmem, vmem, vmem, hbm, hbm, hbm, hbm],
        out_specs=[vmem] * 12,
        scratch_shapes=[
            scratch(*blocks), scratch(WIDTH, QKV_COLS), scratch(TOKENS, WIDTH), scratch(WIDTH, FFN), scratch(FFN, WIDTH),
        ] + [scratch(*blocks)] * 3 + [
            scratch(4, 4, 2, BLOCKS, WIDTH), scratch(4, 4, BLOCKS, WIDTH), scratch(4, 4, BLOCKS, WIDTH), scratch(4, 3, BLOCKS, WIDTH), scratch(4, 3, BLOCKS, WIDTH),
            scratch(4, 2, BLOCKS, WIDTH // 2), scratch(4, 2, BLOCKS, WIDTH // 2),
            scratch(TOKENS, QKV_COLS), scratch(2, TOKENS, TOKENS, dtype=F32), scratch(TOKENS, FFN), scratch(TOKENS, FFN),
            scratch(TOKENS, TOKENS), scratch(BLOCKS, WIDTH), scratch(BLOCKS, WIDTH), scratch(BLOCKS, WIDTH, dtype=F32),
            scratch(BLOCKS, 4, LANES, dtype=F32), scratch(8, 4, LANES, dtype=F32), scratch(4, 4, LANES, dtype=F32), scratch(4, 4, 4, LANES, dtype=F32),
            scratch(BLOCKS, 4, LANES, dtype=F32),
            dma((4, 2, 24)), dma((4, 2, 32)), dma((2, 7)), dma((6,)),
        ],
        compiler_params=pltpu.CompilerParams(collective_id=0, has_side_effects=True, vmem_limit_bytes=LAYER_VMEM),
        name='layer',
    )(
        x_in.reshape(blocks), d_y.reshape(blocks), gain_one, gain_two, seg_ids, w_qkv, w_out.reshape(TOKENS, WIDTH), w_up, w_down,
    )


TILE = 1024


def weight_grad_kernel(
    a, dqkv, o, dr, b1, du, gelu, dy, y, dx, dg1, dg2,
    dwqkv_hbm, dwo_hbm, dw1_hbm, dw2_hbm, y_out, dx_out, dg1_out, dg2_out,
    dwqkv, dwo, dw1, dw2, gelu_t, o_t, out_sems,
):
    stores = []

    def store(src, dst):
        cp = pltpu.make_async_copy(src, dst, out_sems.at[len(stores)])
        cp.start()
        stores.append(cp)

    def by_rows(lhs, rhs, out, out_hbm):
        for i in range(WIDTH // TILE):
            c = pl.ds(i * TILE, TILE)
            out[c, :] = lax.dot_general(lhs[:, c], rhs[...], (((0,), (0,)), ((), ())), preferred_element_type=F32).astype(BF16)
            store(out.at[c], out_hbm.at[c])

    def by_columns(lhs_t, rhs, out, out_hbm):
        for i in range(WIDTH // TILE):
            c = pl.ds(i * TILE, TILE)
            out[:, c] = dot_nn(lhs_t[...], rhs[:, c]).astype(BF16)
            store(out.at[:, c], out_hbm.at[:, c])

    store(y, y_out)
    store(dx, dx_out)
    store(dg1, dg1_out)
    store(dg2, dg2_out)
    by_rows(a, dqkv, dwqkv, dwqkv_hbm)
    by_rows(b1, du, dw1, dw1_hbm)
    gelu_t[...] = gelu[...].T
    by_columns(gelu_t, dy, dw2, dw2_hbm)
    o_t[...] = o[...].T
    by_columns(o_t, dr, dwo, dwo_hbm)
    for cp in stores:
        cp.wait()


def weight_grads(*operands):
    hbm = pl.BlockSpec(memory_space=pl.ANY)
    vmem = pl.BlockSpec(memory_space=pltpu.VMEM)
    big = (TOKENS, WIDTH)
    ins = [big, (TOKENS, QKV_COLS), (TOKENS, TOKENS), big, big, (TOKENS, FFN), (TOKENS, FFN), big, big, big, (WIDTH,), (WIDTH,)]
    outs = [(WIDTH, QKV_COLS), big, (WIDTH, FFN), (FFN, WIDTH), big, big, (WIDTH,), (WIDTH,)]
    return pl.pallas_call(
        weight_grad_kernel,
        out_shape=[jax.ShapeDtypeStruct(dims, BF16) for dims in outs],
        in_specs=[vmem] * len(ins),
        out_specs=[hbm] * len(outs),
        scratch_shapes=[pltpu.VMEM(dims, BF16) for dims in outs[:4] + [(FFN, TOKENS), (TOKENS, TOKENS)]] + [pltpu.SemaphoreType.DMA((20,))],
        compiler_params=pltpu.CompilerParams(vmem_limit_bytes=GRADS_VMEM),
        name='weight_grads',
    )(*[v.reshape(dims) for v, dims in zip(operands, ins)])


def solution(mesh):
    def local_step(x_in, seg_ids, gain_one, w_qkv, w_out, gain_two, w_up, w_down, d_y):
        y, d_x, gains_one, gains_two, normed_one, d_qkv, attn_out, d_resid, normed_two, d_up, gelu_out, d_y_here = layer(
            x_in, d_y, gain_one, gain_two, seg_ids, w_qkv, w_out, w_up, w_down)
        d_w_qkv, d_w_out, d_w_up, d_w_down, y_out, d_x_out, d_gain_one, d_gain_two = weight_grads(
            normed_one, d_qkv, attn_out, d_resid, normed_two, d_up, gelu_out, d_y_here, y, d_x, gains_one, gains_two)
        return y_out.reshape(x_in.shape), d_x_out.reshape(x_in.shape), d_w_qkv, d_w_out.reshape(w_out.shape), d_w_up, d_w_down, d_gain_one, d_gain_two

    in_specs = (P('data'), P('data'), P(), P(None, 'model'), P('model'), P(), P(None, 'model'), P('model'), P('data'))
    out_specs = (P('data'), P('data'), P('data', 'model'), P(('data', 'model')), P('data', 'model'), P(('data', 'model')), P('data'), P('data'))
    return jax.shard_map(local_step, mesh=mesh, in_specs=in_specs, out_specs=out_specs, check_vma=False)
```

time: 181 us -> 139 us (0.77)
  matrix products: 19 us -> 0 us
  Pallas kernels: 152 us -> 137 us
  local copies, waits for them, and re-layouts: 9.2 us -> 0 us
    pallas_call x1, Pallas kernels: 152 us -> 128 us  [layer(): pl.pallas_call(layer_kernel, out_shape=[shape(*blocks), shape(*blocks), s...]
    dot_general x4 -> x0, matrix products: 19 us -> none  [weight_grad(): lax.dot_general(a.reshape(256, -1), b.reshape(256, -1), (((0,), (0,)), ((...]
    pallas_call x0 -> x1, Pallas kernels: none -> 9.14 us  [weight_grads(): pl.pallas_call(weight_grad_kernel, out_shape=[jax.ShapeDtypeStruct(dims,...]
    reshape x3 -> x0, local copies, waits for them, and re-layouts: 4.1 us -> none  [the longest x1 1.47 us: layer(): seg_ids.reshape(256, 1)]
    unnamed x18 -> x0, local copies, waits for them, and re-layouts: 3.69 us -> none
where the time goes in v3:
time: 139 us; the launch traced here: 138 us
  Pallas kernels  137 us (99%)
    pallas_call x1, Pallas kernels, layer(): pl.pallas_call(layer_kernel, out_shape=[shape(*blocks), shape(*blocks), s...  128 us
    pallas_call x1, Pallas kernels, weight_grads(): pl.pallas_call(weight_grad_kernel, out_shape=[jax.ShapeDtypeStruct(dims,...  9.14 us

profile of v3, /device:TPU:0, one launch (start us, length us, event | category | flops | bytes accessed | tf_op | source)
XLA Modules:
  0.0 138.2 jit_solution(14447466417150191864)
XLA Ops:
  0.6 128.2 %layer.1 = (bf16[16,16,4096]{2,1,0:T(8,128)(2,1)S(1)}, bf16[16,16,4096]{2,1,0:T(8,128)(2,1)S(1)}, bf16[4096]{0:T(1024)(128)(2,1)S(1)}, bf16[4096]{0:T(1024)(128)...) custom-call(bf16[16,16,4096]{2,1,0:T(8,128)(2,1)} %bitcast.18, ...), custom_call_target="tpu_custom_call" | custom-call | tf_op jit(solution)/shard_map/layer/pallas_call | solution.py:523
  128.9 9.1 %weight_grads.1 = (bf16[4096,768]{1,0:T(8,128)(2,1)}, bf16[256,4096]{1,0:T(8,128)(2,1)}, bf16[4096,896]{1,0:T(8,128)(2,1)}, bf16[896,4096]{1,0:T(8,128)(2,1)}, b...) custom-call(bf16[256,4096]{1,0:T(8,128)(2,1)S(1)} %bitcast.14, ...), custom_call_target="tpu_custom_call" | custom-call | tf_op jit(solution)/shard_map/weight_grads/pallas_call | solution.py:596

commit v4 on v3

--- a/solution.py
+++ b/solution.py
@@ -20,6 +20,8 @@
 FFN = 896
 QKV_COLS = 768
 CHUNKS = WIDTH // CHUNK
+HALF = WIDTH // 2
+CORE_ORDER = [(3, 1), (1, 1), (1, 0), (2, 1), (0, 1), (3, 0), (2, 0), (0, 0)]
 SCALE = LANES ** -0.5
 GELU_A = 0.7978845608028654
 GELU_B = 0.044715
@@ -42,12 +44,30 @@
     return pl.ds(j * CHUNK, CHUNK)
 
 
-def half(h):
-    return pl.ds(h * (WIDTH // 2), WIDTH // 2)
-
-
-def half_spans(h):
-    return [(span(h * (CHUNKS // 2) + j), span(j)) for j in range(CHUNKS // 2)]
+class Exchange:
+    pieces = 2
+
+    def __init__(self, place, sems):
+        self.place, self.sems = place, sems
+        self.all = range(self.pieces)
+        self.low, self.high = self.all[:self.pieces // 2], self.all[self.pieces // 2:]
+        self.width = WIDTH // self.pieces
+
+    def piece(self, h):
+        return pl.ds(h * self.width, self.width)
+
+    def spans(self, h):
+        n = CHUNKS // self.pieces
+        return [span(h * n + j) for j in range(n)]
+
+    def remote(self, src, dst, i, dev):
+        cp = pltpu.make_async_remote_copy(src_ref=src, dst_ref=dst, send_sem=self.sems.at[0], recv_sem=self.sems.at[1 + i], device_id=dev, device_id_type=MESH)
+        cp.start()
+        return cp
+
+    def drain(self):
+        sent = self.whole.at[pl.ds(0, BLOCKS - 1)]
+        pltpu.make_async_copy(sent, sent, self.sems.at[0]).wait()
 
 
 def fold(v):
@@ -84,31 +104,22 @@
         return self.blocks[i, j, k]
 
 
-def remote(src, dst, sems, dev):
-    cp = pltpu.make_async_remote_copy(src_ref=src, dst_ref=dst, send_sem=sems[0], recv_sem=sems[1], device_id=dev, device_id_type=MESH)
-    cp.start()
-    return cp
-
-
-class ReduceScatter:
+class ReduceScatter(Exchange):
     def __init__(self, place, part, bufs, sems):
-        self.place, self.part, self.sems = place, part, sems
+        super().__init__(place, sems)
+        self.part = self.whole = part
         self.buf_core, self.out_y, self.buf_y, self.out_z, self.buf_z, self.out_first, self.buf_first = bufs
         self.core_in, self.y_in, self.z_in, self.first_in = {}, {}, {}, {}
-        self.ready = set()
-
-    def sem(self, i):
-        return self.sems.at[0, i], self.sems.at[1, i]
+        self.ready, self.first_ready = set(), False
 
     def block(self, k, j):
         return self.place.block(0, j, k)
 
     def start(self):
         p = self.place
-        for k in (3, 1, 2, 0):
-            for j in (1, 0):
-                b = p.block(1, j, k)
-                self.core_in[k, j] = remote(self.part.at[b], self.buf_core.at[k, j], self.sem(k * 2 + j), p.partner)
+        for k, j in CORE_ORDER:
+            b = p.block(1, j, k)
+            self.core_in[k, j] = self.remote(self.part.at[b], self.buf_core.at[k, j], k * 2 + j, p.partner)
 
     def core_ready(self, k, j):
         if (k, j) not in self.ready:
@@ -123,102 +134,96 @@
 
     def send_y(self, k, h):
         self.core_ready(k, 1)
-        if (k, h) == (0, 1):
+        with_first = k == 0 and h in self.high
+        if with_first and not self.first_ready:
             self.first_in[1].wait_recv()
-        for c, d in half_spans(h):
+            self.first_ready = True
+        for c in self.spans(h):
             t = self.pair_sum(k, 1, c)
-            if (k, h) == (0, 1):
-                t = t + self.buf_first[1, :, d].astype(F32)
+            if with_first:
+                t = t + self.buf_first[1, :, pl.ds(c.start - HALF, CHUNK)].astype(F32)
             self.out_y[k, :, c] = t.astype(BF16)
-        self.y_in[k, h] = remote(self.out_y.at[k, :, half(h)], self.buf_y.at[k, :, half(h)], self.sem(8 + k * 2 + h), self.place.y_peer)
+        self.y_in[k, h] = self.remote(self.out_y.at[k, :, self.piece(h)], self.buf_y.at[k, :, self.piece(h)], 8 + k * self.pieces + h, self.place.y_peer)
 
     def send_first(self):
         for j in (1, 0):
             self.core_ready(1, j)
-            for c, d in half_spans(1):
-                self.out_first[j, :, d] = self.pair_sum(1, j, c).astype(BF16)
-            self.first_in[j] = remote(self.out_first.at[j], self.buf_first.at[j], self.sem(22 + j), self.place.z_peers[1])
+            for j2 in range(CHUNKS // 2):
+                self.out_first[j, :, span(j2)] = self.pair_sum(1, j, span(CHUNKS // 2 + j2)).astype(BF16)
+            self.first_in[j] = self.remote(self.out_first.at[j], self.buf_first.at[j], 8 + 7 * self.pieces + j, self.place.z_peers[1])
 
     def send_z(self, k, h):
         self.core_ready(k, 0)
         self.y_in[k, h].wait_recv()
         if k == 2:
             self.z_in[3, h].wait_recv()
-        for c, _ in half_spans(h):
+        for c in self.spans(h):
             t = self.chip_sum(k, c)
             if k == 2:
                 t = t + self.buf_z[2, :, c].astype(F32)
             self.out_z[k - 1, :, c] = t.astype(BF16)
-        self.z_in[k, h] = remote(self.out_z.at[k - 1, :, half(h)], self.buf_z.at[k - 1, :, half(h)], self.sem(14 + k * 2 + h), self.place.z_peers[2 if k == 2 else 1])
+        i = 8 + (3 + k) * self.pieces + h
+        self.z_in[k, h] = self.remote(self.out_z.at[k - 1, :, self.piece(h)], self.buf_z.at[k - 1, :, self.piece(h)], i, self.place.z_peers[2 if k == 2 else 1])
 
     def head(self):
-        return [
-            lambda: self.send_y(3, 0), lambda: self.send_y(3, 1), self.send_first, lambda: self.send_y(1, 0),
-            lambda: self.send_y(2, 0), lambda: self.send_y(2, 1), lambda: self.send_y(0, 0),
-        ]
+        y = {(k, h): (lambda k=k, h=h: self.send_y(k, h)) for k in range(4) for h in self.all}
+        return [y[3, 0], y[3, 1], self.send_first, y[1, 0], y[2, 0], y[2, 1], y[0, 0]]
 
     def tail(self):
-        return [
-            lambda: self.send_z(3, 0), lambda: self.send_z(3, 1), lambda: self.send_y(0, 1),
-            lambda: self.send_z(1, 0), lambda: self.send_z(2, 0), lambda: self.send_z(2, 1),
-        ]
+        z = {(k, h): (lambda k=k, h=h: self.send_z(k, h)) for k in range(4) for h in self.all}
+        return [z[3, 0], z[3, 1], lambda: self.send_y(0, 1), z[1, 0], z[2, 0], z[2, 1]]
 
     def finish(self):
         self.core_ready(0, 0)
-        self.y_in[0, 0].wait_recv()
-        self.y_in[0, 1].wait_recv()
+        for h in self.all:
+            self.y_in[0, h].wait_recv()
         self.first_in[0].wait_recv()
-        self.z_in[1, 0].wait_recv()
-        self.z_in[2, 0].wait_recv()
-        self.z_in[2, 1].wait_recv()
+        for h in self.low:
+            self.z_in[1, h].wait_recv()
+        for h in self.all:
+            self.z_in[2, h].wait_recv()
 
     def total(self, j):
         c = span(j)
         near = self.buf_z[0, :, c] if j < CHUNKS // 2 else self.buf_first[0, :, span(j - CHUNKS // 2)]
         return self.chip_sum(0, c) + near.astype(F32) + self.buf_z[1, :, c].astype(F32)
 
-    def drain(self):
-        for group in (self.core_in, self.y_in, self.z_in, self.first_in):
-            for cp in group.values():
-                cp.wait_send()
-
-
-class Gather:
+
+class Gather(Exchange):
     def __init__(self, place, full, sems):
-        self.place, self.full, self.sems = place, full, sems
-        self.z_in, self.y_in, self.core_in, self.last_in, self.sent = {}, {}, {}, {}, []
+        super().__init__(place, sems)
+        self.full = self.whole = full
+        self.z_in, self.y_in, self.core_in, self.last_in = {}, {}, {}, {}
 
     def send(self, j, k, h, i, dev):
         b = self.place.block(0, j, k)
-        ref = self.full.at[b] if h is None else self.full.at[b, :, half(h)]
-        cp = remote(ref, ref, (self.sems.at[0, i], self.sems.at[1, i]), dev)
-        self.sent.append(cp)
-        return cp
+        ref = self.full.at[b] if h is None else self.full.at[b, :, self.piece(h)]
+        return self.remote(ref, ref, i, dev)
 
     def to_core(self, j, k, h):
-        self.core_in[j, k, h] = self.send(j, k, h, 14 + j * 8 + k * 2 + h, self.place.partner)
+        self.core_in[j, k, h] = self.send(j, k, h, (8 + j * 4 + k) * self.pieces + h, self.place.partner)
 
     def to_y(self, k, h):
-        self.y_in[k, h] = self.send(0, k, h, 6 + k * 2 + h, self.place.y_peer)
+        self.y_in[k, h] = self.send(0, k, h, (4 + k) * self.pieces + h, self.place.y_peer)
 
     def to_z(self, k, h):
-        self.z_in[k, h] = self.send(0, 2 if k == 3 else 0, h, (k - 1) * 2 + h, self.place.z_peers[2 if k == 2 else 1])
+        self.z_in[k, h] = self.send(0, 2 if k == 3 else 0, h, k * self.pieces + h, self.place.z_peers[2 if k == 2 else 1])
 
     def start_far(self):
-        for h in (0, 1):
+        for h in self.all:
             self.to_z(2, h)
 
     def start_near(self):
-        for h in (0, 1):
+        for h in self.all:
             self.to_y(0, h)
             self.to_z(1, h)
-        self.core_in[0, 0, None] = self.send(0, 0, None, 30, self.place.partner)
+        self.core_in[0, 0, None] = self.send(0, 0, None, 8 * self.pieces, self.place.partner)
 
     def from_z(self, k, h):
         self.z_in[k, h].wait_recv()
         if k == 2:
             self.to_z(3, h)
-        if (k, h) != (1, 1):
+        if k != 1 or h in self.low:
             self.to_y(k, h)
         self.to_core(0, k, h)
 
@@ -227,34 +232,32 @@
         self.to_core(1, k, h)
 
     def send_last(self):
-        self.last_in[0] = self.send(1, 0, 1, 31, self.place.z_peers[1])
+        for h in self.high:
+            self.last_in[h] = self.send(1, 0, h, h - self.pieces // 2, self.place.z_peers[1])
 
     def from_last(self):
-        self.last_in[0].wait_recv()
-        self.to_core(1, 1, 1)
+        for h in self.high:
+            self.last_in[h].wait_recv()
+            self.to_core(1, 1, h)
 
     def steps(self):
+        y = {(k, h): (lambda k=k, h=h: self.from_y(k, h)) for k in range(4) for h in self.all}
+        z = {(k, h): (lambda k=k, h=h: self.from_z(k, h)) for k in range(4) for h in self.all}
         return [
-            lambda: self.from_y(0, 0), lambda: self.from_z(2, 0), lambda: self.from_y(0, 1), lambda: self.from_z(2, 1), self.send_last,
-            lambda: self.from_z(1, 0), lambda: self.from_z(1, 1), lambda: self.from_y(2, 0), lambda: self.from_y(2, 1), lambda: self.from_z(3, 0),
-            lambda: self.from_y(1, 0), lambda: self.from_z(3, 1), self.from_last, lambda: self.from_y(3, 0), lambda: self.from_y(3, 1),
+            y[0, 0], z[2, 0], y[0, 1], z[2, 1], self.send_last, z[1, 0], z[1, 1], y[2, 0], y[2, 1], z[3, 0],
+            y[1, 0], z[3, 1], self.from_last, y[3, 0], y[3, 1],
         ]
 
     def late_steps(self):
-        near = [lambda: self.from_y(0, 0), lambda: self.from_y(0, 1), lambda: self.from_z(1, 0), lambda: self.from_z(1, 1)]
-        far = [
-            lambda: self.from_z(2, 0), lambda: self.from_z(2, 1), lambda: self.from_y(1, 0), lambda: self.from_z(3, 0), lambda: self.from_z(3, 1),
-            lambda: self.from_y(2, 0), lambda: self.from_y(2, 1), self.from_last, lambda: self.from_y(3, 0), lambda: self.from_y(3, 1),
-        ]
-        return near, far
+        near = [(lambda h=h: self.from_y(0, h)) for h in self.all] + [(lambda h=h: self.from_z(1, h)) for h in self.all]
+        far = [(lambda h=h: self.from_z(2, h)) for h in self.all]
+        end = [(lambda h=h: self.from_y(1, h)) for h in self.low] + [(lambda h=h: self.from_z(3, h)) for h in self.all]
+        end += [(lambda h=h: self.from_y(2, h)) for h in self.all] + [self.from_last] + [(lambda h=h: self.from_y(3, h)) for h in self.all]
+        return near, far, end
 
     def finish(self):
         for cp in self.core_in.values():
             cp.wait_recv()
-
-    def drain(self):
-        for cp in self.sent:
-            cp.wait_send()
 
 
 def run(steps):
@@ -275,11 +278,13 @@
 
     loads = [
         pltpu.make_async_copy(src, dst, in_sems.at[i])
-        for i, (src, dst) in enumerate([(x_hbm, x), (wqkv_hbm, wqkv), (wo_hbm, wo), (dy_hbm, dy), (w2_hbm, w2), (w1_hbm, w1)])
+        for i, (src, dst) in enumerate(
+            [(x_hbm.at[pl.ds(r * 4, 4)], x.at[pl.ds(r * 4, 4)]) for r in range(4)]
+            + [(wqkv_hbm, wqkv), (wo_hbm, wo), (dy_hbm, dy), (w2_hbm, w2), (w1_hbm, w1)])
     ]
-    load_x, load_wqkv, load_wo, load_dy, load_w2, load_w1 = loads
-    load_x.start()
-    load_wqkv.start()
+    load_x, (load_wqkv, load_wo, load_dy, load_w2, load_w1) = loads[:4], loads[4:]
+    for cp in load_x + [load_wqkv]:
+        cp.start()
     barrier = pltpu.get_barrier_semaphore()
     for dev in [place.partner, place.y_peer] + place.z_peers[1:]:
         pl.semaphore_signal(barrier, inc=1, device_id=dev, device_id_type=MESH)
@@ -288,15 +293,11 @@
         bufs = [ref.at[i] for ref in (core_buf, yout_buf, y_buf, zout_buf, z_buf, fout_buf, first_buf)]
         return ReduceScatter(place, part, bufs, rs_sems.at[i])
 
-    rs1, rs3, rsy, rs4 = rs_set(0, part1), rs_set(1, part3), rs_set(2, part_y), rs_set(3, part1)
-    ag1, ag3, agy, ag4 = [Gather(place, ref, ag_sems.at[i]) for i, ref in enumerate((f1, f2, fy, fx))]
+    rs1, rs3, rsy, rs4 = rs_set(0, part1), rs_set(0, part3), rs_set(1, part_y), rs_set(0, part1)
+    ag1, ag3, agy, ag4 = [Gather(place, ref, ag_sems.at[i]) for i, ref in ((0, f1), (0, f2), (1, fy), (0, fx))]
 
     def gain(ref, j):
         return ref[span(j)].astype(F32).reshape(1, CHUNK)
-
-    load_x.wait()
-    for cp in (load_wo, load_dy, load_w2, load_w1):
-        cp.start()
 
     def ln_one(i, carry):
         rows = pl.ds(i * 2, 2)
@@ -306,7 +307,11 @@
             normed = (x[rows, :, c].astype(F32) - mean) * rstd * gain(g1, j)[None]
             a[rows, :, c] = normed.astype(BF16)
         return carry
-    lax.fori_loop(0, 8, ln_one, 0)
+    for r in range(4):
+        load_x[r].wait()
+        lax.fori_loop(r * 2, r * 2 + 2, ln_one, 0)
+    for cp in (load_wo, load_dy, load_w2, load_w1):
+        cp.start()
 
     load_wqkv.wait()
     qkv[...] = dot_nn(a[...].reshape(TOKENS, WIDTH), wqkv[...]).astype(BF16)
@@ -365,6 +370,7 @@
     run(ag1.steps())
     load_w1.wait()
     ag1.finish()
+    rs1.drain()
 
     for lo, n in ((0, 512), (512, 384)):
         c = pl.ds(lo, n)
@@ -419,13 +425,15 @@
         value = (dy[own, :, c].astype(F32) + wide[:, c].astype(BF16).astype(F32)).astype(BF16)
         d_res[:, c] = value
         f2[own, :, c] = value
+    ag1.drain()
     ag3.start_far()
     ag3.start_near()
     steps = ag3.steps()
-    run(steps[:12])
+    last = steps.index(ag3.from_last)
+    run(steps[:last])
     run(y_head[4:])
     run(y_tail[:2])
-    run(steps[12:])
+    run(steps[last:])
     ag3.finish()
 
     d_attn[...] = dot_nt(f2[...].reshape(TOKENS, WIDTH), wo[...]).astype(BF16)
@@ -440,7 +448,7 @@
         dqkv[:, pl.ds(h * 384 + LANES, LANES)] = dot_nn(d_score.T.astype(BF16), q).astype(BF16)
         dqkv[:, pl.ds(h * 384 + TOKENS, LANES)] = dot_nn(p.T.astype(BF16), d_o).astype(BF16)
     run(y_tail[5:])
-    rs1.drain()
+    rs3.drain()
     project(dqkv, wqkv, part1, WO_TILE, True)
 
     rs4.start()
@@ -460,51 +468,52 @@
     dg_copies = []
 
     def dg_send(src, dst, i, dev):
-        cp = remote(src, dst, (dg_sems.at[0, i], dg_sems.at[1, i]), dev)
+        cp = pltpu.make_async_remote_copy(src_ref=src, dst_ref=dst, send_sem=dg_sems.at[0, i], recv_sem=dg_sems.at[1, i], device_id=dev, device_id_type=MESH)
+        cp.start()
         dg_copies.append(cp)
         return cp
     in_core = dg_send(dg_part.at[pl.ds((1 - place.core) * 8, 8)], dg_core, 0, place.partner)
+    ag3.drain()
     ag4.start_far()
     agy.start_far()
     ag4.start_near()
     steps = ag4.steps()
-    near, far = agy.late_steps()
+    near, far, end = agy.late_steps()
+    last, mid = steps.index(ag4.from_last), steps.index(ag4.send_last)
     in_core.wait_recv()
     dg_core[...] = dg_core[...] + dg_part[pl.ds(place.core * 8, 8)]
     in_y = dg_send(dg_core.at[pl.ds((1 - place.y) * 4, 4)], dg_y, 6, place.y_peer)
     run(near)
-    run(steps[:5])
+    run(steps[:mid + 1])
     in_y.wait_recv()
     quarter = pl.ds(place.core * 8 + place.y * 4, 4)
     dg_z[place.z] = dg_core[pl.ds(place.y * 4, 4)] + dg_y[...]
     in_z = [dg_send(dg_z.at[place.z], dg_z.at[place.z], k, place.z_peers[k]) for k in (1, 2, 3)]
-    run(steps[5:7])
-    run(far[:2])
+    run(steps[mid + 1:mid + 3])
+    run(far)
     agy.send_last()
-    run(steps[7:10])
-    run(far[2:3])
+    run(steps[mid + 3:last - 2])
+    run(end[:2 // 2])
     for cp in in_z:
         cp.wait_recv()
     dg_full[quarter] = dg_z[0] + dg_z[1] + dg_z[2] + dg_z[3]
     in_y = dg_send(dg_full.at[quarter], dg_full.at[quarter], 4, place.y_peer)
-    run(steps[10:13])
-    run(far[3:6])
+    run(steps[last - 2:last + 1])
+    run(end[2 // 2:2 * 2])
     in_y.wait_recv()
     mine = pl.ds(place.core * 8, 8)
     in_core = dg_send(dg_full.at[mine], dg_full.at[mine], 5, place.partner)
-    run(steps[13:])
+    run(steps[last + 1:])
     in_core.wait_recv()
     for i in range(32):
         for row, out in ((0, dg1_out), (2, dg2_out)):
             out[pl.ds(i * LANES, LANES)] = dg_full[i // 2, row + i % 2].astype(BF16)
     ag4.finish()
-    run(far[6:])
+    run(end[2 * 2:])
     agy.finish()
 
-    for rs in (rs3, rsy, rs4):
-        rs.drain()
-    for ag in (ag1, ag3, agy, ag4):
-        ag.drain()
+    for exchange in (rs4, ag4, rsy, agy):
+        exchange.drain()
     for cp in dg_copies:
         cp.wait_send()
 
@@ -531,13 +540,13 @@
         scratch_shapes=[
             scratch(*blocks), scratch(WIDTH, QKV_COLS), scratch(TOKENS, WIDTH), scratch(WIDTH, FFN), scratch(FFN, WIDTH),
         ] + [scratch(*blocks)] * 3 + [
-            scratch(4, 4, 2, BLOCKS, WIDTH), scratch(4, 4, BLOCKS, WIDTH), scratch(4, 4, BLOCKS, WIDTH), scratch(4, 3, BLOCKS, WIDTH), scratch(4, 3, BLOCKS, WIDTH),
-            scratch(4, 2, BLOCKS, WIDTH // 2), scratch(4, 2, BLOCKS, WIDTH // 2),
+            scratch(2, 4, 2, BLOCKS, WIDTH), scratch(2, 4, BLOCKS, WIDTH), scratch(2, 4, BLOCKS, WIDTH), scratch(2, 3, BLOCKS, WIDTH), scratch(2, 3, BLOCKS, WIDTH),
+            scratch(2, 2, BLOCKS, HALF), scratch(2, 2, BLOCKS, HALF),
             scratch(TOKENS, QKV_COLS), scratch(2, TOKENS, TOKENS, dtype=F32), scratch(TOKENS, FFN), scratch(TOKENS, FFN),
             scratch(TOKENS, TOKENS), scratch(BLOCKS, WIDTH), scratch(BLOCKS, WIDTH), scratch(BLOCKS, WIDTH, dtype=F32),
             scratch(BLOCKS, 4, LANES, dtype=F32), scratch(8, 4, LANES, dtype=F32), scratch(4, 4, LANES, dtype=F32), scratch(4, 4, 4, LANES, dtype=F32),
             scratch(BLOCKS, 4, LANES, dtype=F32),
-            dma((4, 2, 24)), dma((4, 2, 32)), dma((2, 7)), dma((6,)),
+            dma((2, 11 + 7 * ReduceScatter.pieces)), dma((2, 1 + BLOCKS * Gather.pieces)), dma((2, 7)), dma((9,)),
         ],
         compiler_params=pltpu.CompilerParams(collective_id=0, has_side_effects=True, vmem_limit_bytes=LAYER_VMEM),
         name='layer',

time: 139 us -> 136 us (0.978)
  Pallas kernels: 137 us -> 135 us
    pallas_call x1, Pallas kernels: 128 us -> 125 us  [layer(): pl.pallas_call(layer_kernel, out_shape=[shape(*blocks), shape(*blocks), s...]
where the time goes in v4:
time: 136 us; the launch traced here: 135 us
  Pallas kernels  135 us (99%)
    pallas_call x1, Pallas kernels, layer(): pl.pallas_call(layer_kernel, out_shape=[shape(*blocks), shape(*blocks), s...  125 us
    pallas_call x1, Pallas kernels, weight_grads(): pl.pallas_call(weight_grad_kernel, out_shape=[jax.ShapeDtypeStruct(dims,...  9.14 us

profile of v4, /device:TPU:0, one launch (start us, length us, event | category | flops | bytes accessed | tf_op | source)
XLA Modules:
  0.0 135.4 jit_solution(9273521942340182632)
XLA Ops:
  0.6 125.4 %layer.1 = (bf16[16,16,4096]{2,1,0:T(8,128)(2,1)S(1)}, bf16[16,16,4096]{2,1,0:T(8,128)(2,1)S(1)}, bf16[4096]{0:T(1024)(128)(2,1)S(1)}, bf16[4096]{0:T(1024)(128)...) custom-call(bf16[16,16,4096]{2,1,0:T(8,128)(2,1)} %bitcast.18, ...), custom_call_target="tpu_custom_call" | custom-call | tf_op jit(solution)/shard_map/layer/pallas_call | solution.py:532
  126.1 9.1 %weight_grads.1 = (bf16[4096,768]{1,0:T(8,128)(2,1)}, bf16[256,4096]{1,0:T(8,128)(2,1)}, bf16[4096,896]{1,0:T(8,128)(2,1)}, bf16[896,4096]{1,0:T(8,128)(2,1)}, b...) custom-call(bf16[256,4096]{1,0:T(8,128)(2,1)S(1)} %bitcast.14, ...), custom_call_target="tpu_custom_call" | custom-call | tf_op jit(solution)/shard_map/weight_grads/pallas_call | solution.py:605

commit v5 on v4

--- a/solution.py
+++ b/solution.py
@@ -11,7 +11,6 @@
 F32 = jnp.float32
 WIDTH = 4096
 CHUNK = 512
-WO_TILE = 2048
 LAYER_VMEM = 49 * 2 ** 20
 GRADS_VMEM = 28 * 2 ** 20
 TOKENS = 256
@@ -21,7 +20,7 @@
 QKV_COLS = 768
 CHUNKS = WIDTH // CHUNK
 HALF = WIDTH // 2
-CORE_ORDER = [(3, 1), (1, 1), (1, 0), (2, 1), (0, 1), (3, 0), (2, 0), (0, 0)]
+CORE_ORDER = [(3, 1), (1, 1), (1, 0), (2, 1), (3, 0), (0, 1), (2, 0), (0, 0)]
 SCALE = LANES ** -0.5
 GELU_A = 0.7978845608028654
 GELU_B = 0.044715
@@ -115,16 +114,16 @@
     def block(self, k, j):
         return self.place.block(0, j, k)
 
-    def start(self):
+    def start(self, h):
         p = self.place
         for k, j in CORE_ORDER:
             b = p.block(1, j, k)
-            self.core_in[k, j] = self.remote(self.part.at[b], self.buf_core.at[k, j], k * 2 + j, p.partner)
-
-    def core_ready(self, k, j):
-        if (k, j) not in self.ready:
-            self.core_in[k, j].wait_recv()
-            self.ready.add((k, j))
+            self.core_in[k, j, h] = self.remote(self.part.at[b, :, self.piece(h)], self.buf_core.at[k, j, :, self.piece(h)], (k * 2 + j) * 2 + h, p.partner)
+
+    def core_ready(self, k, j, h):
+        if (k, j, h) not in self.ready:
+            self.core_in[k, j, h].wait_recv()
+            self.ready.add((k, j, h))
 
     def pair_sum(self, k, j, c):
         return self.part[self.block(k, j), :, c].astype(F32) + self.buf_core[k, j, :, c].astype(F32)
@@ -133,7 +132,7 @@
         return self.pair_sum(k, 0, c) + self.buf_y[k, :, c].astype(F32)
 
     def send_y(self, k, h):
-        self.core_ready(k, 1)
+        self.core_ready(k, 1, h)
         with_first = k == 0 and h in self.high
         if with_first and not self.first_ready:
             self.first_in[1].wait_recv()
@@ -143,17 +142,17 @@
             if with_first:
                 t = t + self.buf_first[1, :, pl.ds(c.start - HALF, CHUNK)].astype(F32)
             self.out_y[k, :, c] = t.astype(BF16)
-        self.y_in[k, h] = self.remote(self.out_y.at[k, :, self.piece(h)], self.buf_y.at[k, :, self.piece(h)], 8 + k * self.pieces + h, self.place.y_peer)
+        self.y_in[k, h] = self.remote(self.out_y.at[k, :, self.piece(h)], self.buf_y.at[k, :, self.piece(h)], BLOCKS + k * self.pieces + h, self.place.y_peer)
 
     def send_first(self):
         for j in (1, 0):
-            self.core_ready(1, j)
+            self.core_ready(1, j, 1)
             for j2 in range(CHUNKS // 2):
                 self.out_first[j, :, span(j2)] = self.pair_sum(1, j, span(CHUNKS // 2 + j2)).astype(BF16)
-            self.first_in[j] = self.remote(self.out_first.at[j], self.buf_first.at[j], 8 + 7 * self.pieces + j, self.place.z_peers[1])
+            self.first_in[j] = self.remote(self.out_first.at[j], self.buf_first.at[j], BLOCKS + 7 * self.pieces + j, self.place.z_peers[1])
 
     def send_z(self, k, h):
-        self.core_ready(k, 0)
+        self.core_ready(k, 0, h)
         self.y_in[k, h].wait_recv()
         if k == 2:
             self.z_in[3, h].wait_recv()
@@ -162,20 +161,20 @@
             if k == 2:
                 t = t + self.buf_z[2, :, c].astype(F32)
             self.out_z[k - 1, :, c] = t.astype(BF16)
-        i = 8 + (3 + k) * self.pieces + h
+        i = BLOCKS + (3 + k) * self.pieces + h
         self.z_in[k, h] = self.remote(self.out_z.at[k - 1, :, self.piece(h)], self.buf_z.at[k - 1, :, self.piece(h)], i, self.place.z_peers[2 if k == 2 else 1])
 
     def head(self):
         y = {(k, h): (lambda k=k, h=h: self.send_y(k, h)) for k in range(4) for h in self.all}
-        return [y[3, 0], y[3, 1], self.send_first, y[1, 0], y[2, 0], y[2, 1], y[0, 0]]
+        return [y[3, 0], y[3, 1], self.send_first, y[2, 0], y[2, 1], y[1, 0], y[0, 0]]
 
     def tail(self):
         z = {(k, h): (lambda k=k, h=h: self.send_z(k, h)) for k in range(4) for h in self.all}
-        return [z[3, 0], z[3, 1], lambda: self.send_y(0, 1), z[1, 0], z[2, 0], z[2, 1]]
+        return [z[3, 0], z[3, 1], lambda: self.send_y(0, 1), z[2, 0], z[2, 1], z[1, 0]]
 
     def finish(self):
-        self.core_ready(0, 0)
         for h in self.all:
+            self.core_ready(0, 0, h)
             self.y_in[0, h].wait_recv()
         self.first_in[0].wait_recv()
         for h in self.low:
@@ -255,9 +254,10 @@
         end += [(lambda h=h: self.from_y(2, h)) for h in self.all] + [self.from_last] + [(lambda h=h: self.from_y(3, h)) for h in self.all]
         return near, far, end
 
-    def finish(self):
-        for cp in self.core_in.values():
-            cp.wait_recv()
+    def finish(self, h=None):
+        for (_, _, at), cp in self.core_in.items():
+            if h is None or (at or 0) == h:
+                cp.wait_recv()
 
 
 def run(steps):
@@ -270,7 +270,7 @@
     fy, fx, dg1_out, dg2_out, a, dqkv, o, f2, f1, d_up, gelu, dy,
     x, wqkv, wo, w1, w2, part1, part3, part_y,
     core_buf, yout_buf, y_buf, zout_buf, z_buf, fout_buf, first_buf,
-    qkv, prob, up, d_gelu, d_attn, x1, d_res, wide, dg_part, dg_core, dg_y, dg_z, dg_full,
+    qkv, prob, up, wide_up, d_gelu, d_attn, x1, d_res, wide, dg_part, dg_core, dg_y, dg_z, dg_full,
     rs_sems, ag_sems, dg_sems, in_sems,
 ):
     place = Place()
@@ -280,10 +280,11 @@
         pltpu.make_async_copy(src, dst, in_sems.at[i])
         for i, (src, dst) in enumerate(
             [(x_hbm.at[pl.ds(r * 4, 4)], x.at[pl.ds(r * 4, 4)]) for r in range(4)]
-            + [(wqkv_hbm, wqkv), (wo_hbm, wo), (dy_hbm, dy), (w2_hbm, w2), (w1_hbm, w1)])
+            + [(wqkv_hbm.at[pl.ds(r * 1024, 1024)], wqkv.at[pl.ds(r * 1024, 1024)]) for r in range(4)]
+            + [(wo_hbm, wo), (dy_hbm, dy), (w2_hbm, w2), (w1_hbm, w1)])
     ]
-    load_x, (load_wqkv, load_wo, load_dy, load_w2, load_w1) = loads[:4], loads[4:]
-    for cp in load_x + [load_wqkv]:
+    load_x, load_wqkv, (load_wo, load_dy, load_w2, load_w1) = loads[:4], loads[4:8], loads[8:]
+    for cp in load_x + load_wqkv:
         cp.start()
     barrier = pltpu.get_barrier_semaphore()
     for dev in [place.partner, place.y_peer] + place.z_peers[1:]:
@@ -313,7 +314,8 @@
     for cp in (load_wo, load_dy, load_w2, load_w1):
         cp.start()
 
-    load_wqkv.wait()
+    for cp in load_wqkv:
+        cp.wait()
     qkv[...] = dot_nn(a[...].reshape(TOKENS, WIDTH), wqkv[...]).astype(BF16)
 
     q_pos = lax.broadcasted_iota(jnp.int32, (TOKENS, TOKENS), 0)
@@ -337,10 +339,12 @@
         lax.fori_loop(0, (hi - lo) // tile, step, 0)
 
     load_wo.wait()
-    project(o, wo, part1, WO_TILE, False)
     pl.semaphore_wait(barrier, 5)
-
-    rs1.start()
+    project(o, wo, part1, HALF, False, 0, HALF)
+    rs1.start(0)
+    project(o, wo, part1, HALF, False, HALF)
+
+    rs1.start(1)
     run(rs1.head())
 
     def d_gelu_tile(lo, n):
@@ -350,11 +354,10 @@
     load_w2.wait()
     tail = rs1.tail()
     d_gelu_tile(0, TOKENS)
-    run(tail[:4])
     d_gelu_tile(TOKENS, TOKENS)
-    run(tail[4:5])
+    run(tail[:3])
     d_gelu_tile(512, TOKENS)
-    run(tail[5:])
+    run(tail[3:])
     d_gelu_tile(QKV_COLS, LANES)
     rs1.finish()
 
@@ -369,12 +372,12 @@
     ag1.start_near()
     run(ag1.steps())
     load_w1.wait()
-    ag1.finish()
+    left, right = pl.ds(0, HALF), pl.ds(HALF, HALF)
+    ag1.finish(0)
+    wide_up[...] = dot_nn(f1[:, :, left].reshape(TOKENS, HALF), w1[left, :])
+    ag1.finish(1)
     rs1.drain()
-
-    for lo, n in ((0, 512), (512, 384)):
-        c = pl.ds(lo, n)
-        up[:, c] = dot_nn(f1[...].reshape(TOKENS, WIDTH), w1[:, c]).astype(BF16)
+    up[...] = (wide_up[...] + dot_nn(f1[:, :, right].reshape(TOKENS, HALF), w1[right, :])).astype(BF16)
 
     def activation(i, carry):
         rows = pl.ds(pl.multiple_of(i * BLOCKS, BLOCKS), BLOCKS)
@@ -385,17 +388,21 @@
         d_up[rows, :] = (d_gelu[rows, :].astype(F32) * slope).astype(BF16)
         return carry
     lax.fori_loop(0, BLOCKS, activation, 0)
-    project(d_up, w1, part3, WO_TILE, True)
-
-    rs3.start()
+    project(d_up, w1, part3, HALF, True, 0, HALF)
+    rs3.start(0)
+    project(d_up, w1, part3, HALF, True, HALF)
+
+    rs3.start(1)
     run(rs3.head())
     tail, y_head, y_tail = rs3.tail(), rsy.head(), rsy.tail()
-    project(gelu, w2, part_y, 1024, False, 0, 2048)
-    run(tail[:4])
-    project(gelu, w2, part_y, 1024, False, 2048, 4096)
-    rsy.start()
-    run(tail[4:])
-    run(y_head[:4])
+    project(gelu, w2, part_y, HALF, False, 0, HALF)
+    rsy.start(0)
+    project(gelu, w2, part_y, HALF, False, HALF)
+    rsy.start(1)
+    run(tail[:5])
+    run(y_head[:2])
+    run(tail[5:])
+    run(y_head[2:4])
     rs3.finish()
 
     def ln_backward(rs, z, mean, rstd, gain_ref, dg_row):
@@ -434,9 +441,10 @@
     run(y_head[4:])
     run(y_tail[:2])
     run(steps[last:])
-    ag3.finish()
-
-    d_attn[...] = dot_nt(f2[...].reshape(TOKENS, WIDTH), wo[...]).astype(BF16)
+    ag3.finish(0)
+    wide_attn = dot_nt(f2[:, :, left].reshape(TOKENS, HALF), wo[:, left])
+    ag3.finish(1)
+    d_attn[...] = (wide_attn + dot_nt(f2[:, :, right].reshape(TOKENS, HALF), wo[:, right])).astype(BF16)
     run(y_tail[2:5])
     for h in range(2):
         q, k, v = [qkv[:, pl.ds(h * 384 + i * LANES, LANES)] for i in range(3)]
@@ -449,15 +457,19 @@
         dqkv[:, pl.ds(h * 384 + TOKENS, LANES)] = dot_nn(p.T.astype(BF16), d_o).astype(BF16)
     run(y_tail[5:])
     rs3.drain()
-    project(dqkv, wqkv, part1, WO_TILE, True)
-
-    rs4.start()
+    project(dqkv, wqkv, part1, HALF, True, 0, HALF)
+    rs4.start(0)
+    project(dqkv, wqkv, part1, HALF, True, HALF)
+
+    rs4.start(1)
     run(rs4.head())
+    tail = rs4.tail()
+    run(tail[:3])
     rsy.finish()
     for j in range(CHUNKS):
         c = span(j)
         fy[own, :, c] = (x1[:, c].astype(F32) + rsy.total(j)).astype(BF16)
-    run(rs4.tail())
+    run(tail[3:])
     agy.start_near()
     rs4.finish()
     mean1, rstd1 = row_stats(lambda j: x[own, :, span(j)].astype(F32))
@@ -542,11 +554,11 @@
         ] + [scratch(*blocks)] * 3 + [
             scratch(2, 4, 2, BLOCKS, WIDTH), scratch(2, 4, BLOCKS, WIDTH), scratch(2, 4, BLOCKS, WIDTH), scratch(2, 3, BLOCKS, WIDTH), scratch(2, 3, BLOCKS, WIDTH),
             scratch(2, 2, BLOCKS, HALF), scratch(2, 2, BLOCKS, HALF),
-            scratch(TOKENS, QKV_COLS), scratch(2, TOKENS, TOKENS, dtype=F32), scratch(TOKENS, FFN), scratch(TOKENS, FFN),
+            scratch(TOKENS, QKV_COLS), scratch(2, TOKENS, TOKENS, dtype=F32), scratch(TOKENS, FFN), scratch(TOKENS, FFN, dtype=F32), scratch(TOKENS, FFN),
             scratch(TOKENS, TOKENS), scratch(BLOCKS, WIDTH), scratch(BLOCKS, WIDTH), scratch(BLOCKS, WIDTH, dtype=F32),
             scratch(BLOCKS, 4, LANES, dtype=F32), scratch(8, 4, LANES, dtype=F32), scratch(4, 4, LANES, dtype=F32), scratch(4, 4, 4, LANES, dtype=F32),
             scratch(BLOCKS, 4, LANES, dtype=F32),
-            dma((2, 11 + 7 * ReduceScatter.pieces)), dma((2, 1 + BLOCKS * Gather.pieces)), dma((2, 7)), dma((9,)),
+            dma((2, BLOCKS + 3 + 7 * ReduceScatter.pieces)), dma((2, 1 + BLOCKS * Gather.pieces)), dma((2, 7)), dma((12,)),
         ],
         compiler_params=pltpu.CompilerParams(collective_id=0, has_side_effects=True, vmem_limit_bytes=LAYER_VMEM),
         name='layer',

time: 136 us -> 135 us (level)
  no operation moved by 1% of the time
where the time goes in v5:
time: 135 us
  Pallas kernels  134 us (99%)
    pallas_call x1, Pallas kernels, layer(): pl.pallas_call(layer_kernel, out_shape=[shape(*blocks), shape(*blocks), s...  125 us
    pallas_call x1, Pallas kernels, weight_grads(): pl.pallas_call(weight_grad_kernel, out_shape=[jax.ShapeDtypeStruct(dims,...  9.14 us

profile of v5, /device:TPU:0, one launch (start us, length us, event | category | flops | bytes accessed | tf_op | source)
XLA Modules:
  0.0 134.9 jit_solution(4240343736432117992)
XLA Ops:
  0.6 124.9 %layer.1 = (bf16[16,16,4096]{2,1,0:T(8,128)(2,1)S(1)}, bf16[16,16,4096]{2,1,0:T(8,128)(2,1)S(1)}, bf16[4096]{0:T(1024)(128)(2,1)S(1)}, bf16[4096]{0:T(1024)(128)...) custom-call(bf16[16,16,4096]{2,1,0:T(8,128)(2,1)} %bitcast.18, ...), custom_call_target="tpu_custom_call" | custom-call | tf_op jit(solution)/shard_map/layer/pallas_call | solution.py:544
  125.5 9.1 %weight_grads.1 = (bf16[4096,768]{1,0:T(8,128)(2,1)}, bf16[256,4096]{1,0:T(8,128)(2,1)}, bf16[4096,896]{1,0:T(8,128)(2,1)}, bf16[896,4096]{1,0:T(8,128)(2,1)}, b...) custom-call(bf16[256,4096]{1,0:T(8,128)(2,1)S(1)} %bitcast.14, ...), custom_call_target="tpu_custom_call" | custom-call | tf_op jit(solution)/shard_map/weight_grads/pallas_call | solution.py:617

commit v6 on v5

--- a/solution.py
+++ b/solution.py
@@ -300,23 +300,26 @@
     def gain(ref, j):
         return ref[span(j)].astype(F32).reshape(1, CHUNK)
 
-    def ln_one(i, carry):
-        rows = pl.ds(i * 2, 2)
+    def ln_one(i):
+        rows = pl.ds(i * 4, 4)
         mean, rstd = row_stats(lambda j: x[rows, :, span(j)].astype(F32))
         for j in range(CHUNKS):
             c = span(j)
             normed = (x[rows, :, c].astype(F32) - mean) * rstd * gain(g1, j)[None]
             a[rows, :, c] = normed.astype(BF16)
-        return carry
     for r in range(4):
         load_x[r].wait()
-        lax.fori_loop(r * 2, r * 2 + 2, ln_one, 0)
+        ln_one(r)
     for cp in (load_wo, load_dy, load_w2, load_w1):
         cp.start()
 
-    for cp in load_wqkv:
+    left, right = pl.ds(0, HALF), pl.ds(HALF, HALF)
+    for cp in load_wqkv[:2]:
         cp.wait()
-    qkv[...] = dot_nn(a[...].reshape(TOKENS, WIDTH), wqkv[...]).astype(BF16)
+    wide_up[:, pl.ds(0, QKV_COLS)] = dot_nn(a[:, :, left].reshape(TOKENS, HALF), wqkv[left, :])
+    for cp in load_wqkv[2:]:
+        cp.wait()
+    qkv[...] = (wide_up[:, pl.ds(0, QKV_COLS)] + dot_nn(a[:, :, right].reshape(TOKENS, HALF), wqkv[right, :])).astype(BF16)
 
     q_pos = lax.broadcasted_iota(jnp.int32, (TOKENS, TOKENS), 0)
     k_pos = lax.broadcasted_iota(jnp.int32, (TOKENS, TOKENS), 1)
@@ -372,7 +375,6 @@
     ag1.start_near()
     run(ag1.steps())
     load_w1.wait()
-    left, right = pl.ds(0, HALF), pl.ds(HALF, HALF)
     ag1.finish(0)
     wide_up[...] = dot_nn(f1[:, :, left].reshape(TOKENS, HALF), w1[left, :])
     ag1.finish(1)
@@ -380,14 +382,14 @@
     up[...] = (wide_up[...] + dot_nn(f1[:, :, right].reshape(TOKENS, HALF), w1[right, :])).astype(BF16)
 
     def activation(i, carry):
-        rows = pl.ds(pl.multiple_of(i * BLOCKS, BLOCKS), BLOCKS)
+        rows = pl.ds(pl.multiple_of(i * 32, 32), 32)
         u = up[rows, :].astype(F32)
         t = jnp.tanh(GELU_A * (u + GELU_B * (u * u * u)))
         gelu[rows, :] = (0.5 * u * (1.0 + t)).astype(BF16)
         slope = 0.5 * (1.0 + t) + 0.5 * u * (1.0 - t * t) * (GELU_A * (1.0 + 3.0 * GELU_B * (u * u)))
         d_up[rows, :] = (d_gelu[rows, :].astype(F32) * slope).astype(BF16)
         return carry
-    lax.fori_loop(0, BLOCKS, activation, 0)
+    lax.fori_loop(0, 8, activation, 0)
     project(d_up, w1, part3, HALF, True, 0, HALF)
     rs3.start(0)
     project(d_up, w1, part3, HALF, True, HALF)
@@ -402,7 +404,7 @@
     run(tail[:5])
     run(y_head[:2])
     run(tail[5:])
-    run(y_head[2:4])
+    run(y_head[2:5])
     rs3.finish()
 
     def ln_backward(rs, z, mean, rstd, gain_ref, dg_row):
@@ -438,7 +440,7 @@
     steps = ag3.steps()
     last = steps.index(ag3.from_last)
     run(steps[:last])
-    run(y_head[4:])
+    run(y_head[5:])
     run(y_tail[:2])
     run(steps[last:])
     ag3.finish(0)

time: 135 us -> 134 us (level)
  Pallas kernels: 134 us -> 132 us
    pallas_call x1, Pallas kernels: 125 us -> 123 us  [layer(): pl.pallas_call(layer_kernel, out_shape=[shape(*blocks), shape(*blocks), s...]
where the time goes in v6:
time: 134 us; the launch traced here: 133 us
  Pallas kernels  132 us (99%)
    pallas_call x1, Pallas kernels, layer(): pl.pallas_call(layer_kernel, out_shape=[shape(*blocks), shape(*blocks), s...  123 us
    pallas_call x1, Pallas kernels, weight_grads(): pl.pallas_call(weight_grad_kernel, out_shape=[jax.ShapeDtypeStruct(dims,...  9.14 us

profile of v6, /device:TPU:0, one launch (start us, length us, event | category | flops | bytes accessed | tf_op | source)
XLA Modules:
  0.0 133.3 jit_solution(97106330659059464)
XLA Ops:
  0.6 123.3 %layer.1 = (bf16[16,16,4096]{2,1,0:T(8,128)(2,1)S(1)}, bf16[16,16,4096]{2,1,0:T(8,128)(2,1)S(1)}, bf16[4096]{0:T(1024)(128)(2,1)S(1)}, bf16[4096]{0:T(1024)(128)...) custom-call(bf16[16,16,4096]{2,1,0:T(8,128)(2,1)} %bitcast.18, ...), custom_call_target="tpu_custom_call" | custom-call | tf_op jit(solution)/shard_map/layer/pallas_call | solution.py:546
  124.0 9.1 %weight_grads.1 = (bf16[4096,768]{1,0:T(8,128)(2,1)}, bf16[256,4096]{1,0:T(8,128)(2,1)}, bf16[4096,896]{1,0:T(8,128)(2,1)}, bf16[896,4096]{1,0:T(8,128)(2,1)}, b...) custom-call(bf16[256,4096]{1,0:T(8,128)(2,1)S(1)} %bitcast.14, ...), custom_call_target="tpu_custom_call" | custom-call | tf_op jit(solution)/shard_map/weight_grads/pallas_call | solution.py:619

commit v7 on v6

--- a/solution.py
+++ b/solution.py
@@ -404,7 +404,7 @@
     run(tail[:5])
     run(y_head[:2])
     run(tail[5:])
-    run(y_head[2:5])
+    run(y_head[2:6])
     rs3.finish()
 
     def ln_backward(rs, z, mean, rstd, gain_ref, dg_row):
@@ -440,7 +440,7 @@
     steps = ag3.steps()
     last = steps.index(ag3.from_last)
     run(steps[:last])
-    run(y_head[5:])
+    run(y_head[6:])
     run(y_tail[:2])
     run(steps[last:])
     ag3.finish(0)
@@ -518,12 +518,12 @@
     mine = pl.ds(place.core * 8, 8)
     in_core = dg_send(dg_full.at[mine], dg_full.at[mine], 5, place.partner)
     run(steps[last + 1:])
+    run(end[2 * 2:])
     in_core.wait_recv()
     for i in range(32):
         for row, out in ((0, dg1_out), (2, dg2_out)):
             out[pl.ds(i * LANES, LANES)] = dg_full[i // 2, row + i % 2].astype(BF16)
     ag4.finish()
-    run(end[2 * 2:])
     agy.finish()
 
     for exchange in (rs4, ag4, rsy, agy):

time: 134 us -> 134 us (level)
  no operation moved by 1% of the time
where the time goes in v7:
time: 134 us
  Pallas kernels  133 us (99%)
    pallas_call x1, Pallas kernels, layer(): pl.pallas_call(layer_kernel, out_shape=[shape(*blocks), shape(*blocks), s...  124 us
    pallas_call x1, Pallas kernels, weight_grads(): pl.pallas_call(weight_grad_kernel, out_shape=[jax.ShapeDtypeStruct(dims,...  9.14 us

profile of v7, /device:TPU:0, one launch (start us, length us, event | category | flops | bytes accessed | tf_op | source)
XLA Modules:
  0.0 134.0 jit_solution(15711156437588604659)
XLA Ops:
  0.6 124.1 %layer.1 = (bf16[16,16,4096]{2,1,0:T(8,128)(2,1)S(1)}, bf16[16,16,4096]{2,1,0:T(8,128)(2,1)S(1)}, bf16[4096]{0:T(1024)(128)(2,1)S(1)}, bf16[4096]{0:T(1024)(128)...) custom-call(bf16[16,16,4096]{2,1,0:T(8,128)(2,1)} %bitcast.18, ...), custom_call_target="tpu_custom_call" | custom-call | tf_op jit(solution)/shard_map/layer/pallas_call | solution.py:546
  124.7 9.1 %weight_grads.1 = (bf16[4096,768]{1,0:T(8,128)(2,1)}, bf16[256,4096]{1,0:T(8,128)(2,1)}, bf16[4096,896]{1,0:T(8,128)(2,1)}, bf16[896,4096]{1,0:T(8,128)(2,1)}, b...) custom-call(bf16[256,4096]{1,0:T(8,128)(2,1)S(1)} %bitcast.14, ...), custom_call_target="tpu_custom_call" | custom-call | tf_op jit(solution)/shard_map/weight_grads/pallas_call | solution.py:619
